TPU v7x, 32 devices: a whole 2x2x4 slice. The times are simulated.
32 devices in a mesh: gx: 4 (over z), gy: 2 (over y), gz: 4 (over x, core).
Axes of the slice: x: 2, y: 2, z: 4, core: 2. Of those that a mesh axis runs over, the one named last changes fastest.
Arguments:
- displacement: float32 [3, 64, 64, 1024], P(None, 'gx', 'gy', 'gz'), may hold values from -1.5 to 1.5
- density: float32 [64, 64, 1024], P('gx', 'gy', 'gz'), may hold values from 0.03 to 1
- stiffness: float32 [24, 24], replicated, may hold values from -9 to 9.5, as said below
Outputs:
- filtered: float32 [64, 64, 1024], P('gx', 'gy', 'gz')
- compliance: float32 [], replicated
- volume: float32 [], replicated
Inputs may be any that keep to these rules, and one draw needn't show every extreme that they name: `stiffness`: symmetric and positive definite, every eigenvalue at least 0.5.
All inputs are finite; a program needn't handle non-finite values.
Results may differ from a plain program's by a relative error of at most 0.00005.
Values sent between devices are 32-bit elements; how exact they have to be, the bound alone decides.
A program may use at most 64 MiB of HBM per device.

v0:
```python
import functools

import jax
import jax.numpy as jnp
from jax import lax
from jax.experimental import pallas as pl
from jax.experimental.pallas import tpu as pltpu
from jax.sharding import PartitionSpec as P

VOID = 0.001
H = (1.0, 2.0, 3.0, 2.0, 1.0)
MESH = pl.DeviceIdType.MESH
AXES = ("gx", "gy", "gz")
F32 = jnp.float32
BF16 = jnp.bfloat16
NODE_STEPS = [(a, b, c) for a in (0, 1) for b in (0, 1) for c in (0, 1) if a + b + c]
SIDE_STEPS = [(b, c) for b in (-1, 0, 1) for c in (-1, 0, 1) if b or c]


def iota(shape, dim):
    return lax.broadcasted_iota(jnp.int32, shape, dim)


def line_sum(position, extent):
    total = None
    for d in range(5):
        at = position + (d - 2)
        term = jnp.where((at >= 0) & (at < extent), H[d], 0.0).astype(F32)
        total = term if total is None else total + term
    return total


def band_weights(stiff):
    rows, cols = 192, 256
    pick = jnp.where((iota((rows, 24), 0) >> 3) == iota((rows, 24), 1), 1.0, 0.0).astype(F32)

    def column(shape):
        col = iota(shape, 1)
        a, g, s = col >> 7, (col >> 4) & 7, col & 7
        cm = jnp.where(g == 6, s, g)
        c = jnp.where(cm >= 3, 1, 0)
        m = cm - 3 * c
        valid = (g < 6) | ((g == 6) & (s < 6))
        return 8 * m + 4 * a + c, valid, jnp.where(g == 6, 8, s), (col >> 3) & 1

    total = None
    for b in (0, 1):
        q, valid, _, _ = column((24, cols))
        place = jnp.where((iota((24, cols), 0) == q + 2 * b) & valid, 1.0, 0.0).astype(F32)
        wide = jnp.dot(stiff, place, precision=lax.Precision.HIGHEST, preferred_element_type=F32)
        tall = jnp.dot(pick, wide, precision=lax.Precision.HIGHEST, preferred_element_type=F32)
        _, _, jj, _ = column((rows, cols))
        term = jnp.where(jj - (iota((rows, cols), 0) & 7) == b, tall, 0.0)
        total = term if total is None else total + term
    high = total.astype(BF16).astype(F32)
    _, _, _, lo_col = column((rows, cols))
    low = jnp.where(lo_col == 0, total - high, 0.0)
    return high.astype(BF16), low.astype(BF16)


def kernel(
    sizes, u_hbm, rho_hbm, stiff_hbm, out, packs, totals,
    u, rho, stiff, rx, ry, rxy, rz, ys, yd, zs, field, parts, weights, wx, wy,
    yslo, yshi, rylo, ryhi, zslo, zshi, rzz, sums, insem, nsend, nrecv, fsend, frecv, gsend, grecv,
):
    ni, nj, nk = rho.shape
    n = dict(zip(AXES, sizes))
    me = {axis: lax.axis_index(axis) for axis in AXES}
    ny, nz = n["gy"], n["gz"]
    down = {axis: me[axis] > 0 for axis in AXES}
    up = {axis: me[axis] < n[axis] - 1 for axis in AXES}

    loads = []
    for at, (src, dst) in enumerate(((stiff_hbm, stiff), (u_hbm, u), (rho_hbm, rho))):
        copy = pltpu.make_async_copy(src, dst, insem.at[at])
        copy.start()
        loads.append(copy)

    def hop(step):
        ids, ok = {}, None
        for axis, s in zip(AXES, step):
            if s:
                ids[axis] = me[axis] + s
                flag = up[axis] if s > 0 else down[axis]
                ok = flag if ok is None else jnp.logical_and(ok, flag)
        return ids, ok

    def minus(step):
        return tuple(-s for s in step)

    line = [{"gx": lax.rem(me["gx"] + off, n["gx"])} for off in range(1, n["gx"])]
    sheet = [
        {"gy": lax.rem(me["gy"] + off // nz, ny), "gz": lax.rem(me["gz"] + off % nz, nz)}
        for off in range(1, ny * nz)
    ]
    barrier = pltpu.get_barrier_semaphore()
    for ids in line + sheet:
        pl.semaphore_signal(barrier, inc=1, device_id=ids, device_id_type=MESH)
    peers = len(line) + len(sheet)
    for step in NODE_STEPS:
        if step[0] and sum(step) > 1:
            for way in (step, minus(step)):
                ids, ok = hop(way)
                peers = peers + jnp.where(ok, 1, 0)

                @pl.when(ok)
                def _():
                    pl.semaphore_signal(barrier, inc=1, device_id=ids, device_id_type=MESH)

    pl.semaphore_wait(barrier, peers)

    def swap(copies, src, dst, send_sem, recv_sem, step):
        ids, sends = hop(step)
        copy = pltpu.make_async_remote_copy(
            src_ref=src, dst_ref=dst, send_sem=send_sem, recv_sem=recv_sem,
            device_id=ids, device_id_type=MESH,
        )
        copies.append((copy, sends, hop(minus(step))[1], dst))

        @pl.when(sends)
        def _():
            copy.start()

    def arrive(copies):
        for copy, _, takes, dst in copies:

            @pl.when(takes)
            def _():
                copy.wait_recv()

            @pl.when(jnp.logical_not(takes))
            def _():
                dst[...] = jnp.zeros(dst.shape, F32)

    def finish(copies):
        for copy, sends, _, _ in copies:

            @pl.when(sends)
            def _():
                copy.wait_send()

    beside, below, far = [], [], []

    def node_swap(step):
        a, b, c = step
        at = NODE_STEPS.index(step)
        if c:
            src, dst = (zs.at[0:8], rz.at[a, b, 0:8]) if b else (zs, rz.at[a, b])
        elif b:
            src, dst = (yd, rxy) if a else (ys, ry)
        else:
            src, dst = u_hbm.at[:, 0], rx
        copies = far if a else (below if b else beside)
        swap(copies, src, dst, nsend.at[at], nrecv.at[at], minus(step))

    node_swap((1, 0, 0))
    loads[1].wait()
    lane = iota((nj, 128), 1)
    def pack(i, acc):
        for m in range(3):
            at = m * ni + i
            acc = jnp.where(lane == at, pltpu.roll(u[m, i, :, 0:128], at, 1), acc)
        return acc

    zs[...] = lax.fori_loop(0, ni, pack, jnp.zeros((nj, 128), F32), unroll=4)
    for step in NODE_STEPS:
        if step[2]:
            node_swap(step)
    yd[...] = jnp.zeros(yd.shape, F32)
    for m in range(3):
        for i in range(ni):
            ys[m, i : i + 1, :] = u[m, i, 0:1, :]
        yd[m : m + 1, :] = u[m, 0, 0:1, :]
    node_swap((0, 1, 0))
    node_swap((1, 1, 0))
    loads[0].wait()
    high, low = band_weights(stiff[...])
    weights[0:192, :] = high
    weights[192:384, :] = low

    last = iota((nj, nk), 1) == nk - 1
    last8 = iota((8, nk), 1) == nk - 1
    sub8 = iota((8, nk), 0)

    def split(f):
        hi = f.astype(BF16).astype(F32)
        return jnp.concatenate([hi, f - hi], 0).astype(BF16)

    def put(jt, to, at, f):
        parts[jt, pl.ds(pl.multiple_of(to * 128, 128) + at, 16), :] = split(f)

    def first_half(m, to, base):
        field[0, m, to, 0:nj, :] = base
        for jt in range(nj // 8):
            put(jt, to, 16 * m, base[8 * jt : 8 * jt + 8])

    def second_half(m, to, base, col, at):
        side = pltpu.roll(col, 127 - at, 1)
        moved = jnp.where(last, jnp.concatenate([side, side], 1), pltpu.roll(base, nk - 1, 1))
        field[1, m, to, 0:nj, :] = moved
        for jt in range(nj // 8):
            put(jt, to, 48 + 16 * m, moved[8 * jt : 8 * jt + 8])

    def next_row(m, to, row, corner, at):
        row8 = jnp.broadcast_to(row, (8, nk))
        field[0, m, to, nj : nj + 8, :] = row8
        side8 = pltpu.roll(corner, 127 - at, 1)
        field[1, m, to, nj : nj + 8, :] = jnp.where(
            last8, jnp.concatenate([side8, side8], 1), pltpu.roll(row8, nk - 1, 1)
        )

    def edges(to):
        for jt in range(nj // 8):
            edge = jnp.zeros((8, nk), F32)
            for cm in range(6):
                c, m = divmod(cm, 3)
                row = field[c, m, to, 8 * jt + 8 : 8 * jt + 9, :]
                edge = jnp.where(sub8 == cm, jnp.broadcast_to(row, (8, nk)), edge)
            put(jt, to, 96, edge)

    def own_first(i, carry):
        for m in range(3):
            first_half(m, i, u[m, i])
        for jt in range(nj // 8):
            parts[jt, pl.ds(pl.multiple_of(i * 128, 128) + 112, 16), :] = jnp.zeros((16, nk), BF16)
        return carry

    def own_second(i, carry):
        for m in range(3):
            second_half(m, i, u[m, i], rz[0, 0], m * ni + i)
        return carry

    def own_edges(i, carry):
        for m in range(3):
            next_row(m, i, ry[m, pl.ds(i, 1), :], rz[0, 1, 0:8, :], m * ni + i)
        edges(i)
        return carry

    lax.fori_loop(0, ni, own_first, 0)
    for jt in range(nj // 8):
        parts[jt, ni * 128 + 112 : ni * 128 + 128, :] = jnp.zeros((16, nk), BF16)
    loads[2].wait()
    wy[0, 0:nj, :] = 1.0 / (
        line_sum(me["gy"] * nj + iota((nj, nk), 0), ny * nj)
        * line_sum(me["gz"] * nk + iota((nj, nk), 1), nz * nk)
    )
    arrive(beside)
    lax.fori_loop(0, ni, own_second, 0, unroll=2)
    arrive(below)
    lax.fori_loop(0, ni, own_edges, 0, unroll=2)
    arrive(far)
    for m in range(3):
        first_half(m, ni, rx[m])
        second_half(m, ni, rx[m], rz[1, 0], m * ni)
        next_row(m, ni, rxy[m : m + 1, :], rz[1, 1, 0:8, :], m * ni)
    edges(ni)

    def plane(i, carry):
        c_sum, v_sum = carry
        inv_x = 1.0 / line_sum(jnp.full((8, nk), me["gx"] * ni + i, jnp.int32), n["gx"] * ni)
        for jt in range(nj // 8):
            data = parts[jt, pl.ds(pl.multiple_of(i * 128, 128), 256), :]
            product = jnp.dot(weights[...], data, preferred_element_type=F32)
            energy = None
            for r in range(24):
                m, a, b, c = r >> 3, (r >> 2) & 1, (r >> 1) & 1, r & 1
                v = product[8 * r : 8 * r + 8] + product[192 + 8 * r : 200 + 8 * r]
                term = v * field[c, m, i + a, 8 * jt + b : 8 * jt + b + 8, :]
                energy = term if energy is None else energy + term
            d = rho[i, 8 * jt : 8 * jt + 8, :]
            c_sum = c_sum + (VOID + d * d * d * (1.0 - VOID)) * energy
            v_sum = v_sum + d
            wx[i + 2, 8 * jt : 8 * jt + 8, :] = (
                (-3.0 * (1.0 - VOID)) * d * d * energy * (inv_x * wy[0, 8 * jt : 8 * jt + 8, :])
            )
        return c_sum, v_sum

    zero = jnp.zeros((8, nk), F32)
    carry = lax.fori_loop(
        0, 4, lambda t, s: plane(jnp.where(t < 2, t, ni - 4 + t), s), (zero, zero)
    )
    x_copies = []
    swap(x_copies, wx.at[2:4], wx.at[ni + 2 : ni + 4], fsend.at[8], frecv.at[8], (-1, 0, 0))
    swap(x_copies, wx.at[ni : ni + 2], wx.at[0:2], fsend.at[9], frecv.at[9], (1, 0, 0))
    c_sum, v_sum = lax.fori_loop(4, ni, lambda t, s: plane(t - 2, s), carry)

    def share(base, mine, value, group):
        sums[base + mine] = value
        copies = []
        for off, ids in enumerate(group):
            copy = pltpu.make_async_remote_copy(
                src_ref=sums.at[base + mine], dst_ref=sums.at[base + mine],
                send_sem=gsend.at[base + off], recv_sem=grecv.at[base + off],
                device_id=ids, device_id_type=MESH,
            )
            copy.start()
            copies.append(copy)
        return copies

    def gather(base, copies):
        for copy in copies:
            copy.wait()
        total = sums[base]
        for at in range(1, len(copies) + 1):
            total = total + sums[base + at]
        return total


    def fold(x):
        row = jnp.sum(x, axis=0, keepdims=True)
        row = row[:, :128] + row[:, 128:]
        return row + pltpu.roll(row, 64, 1)

    partial = jnp.where(iota((1, 128), 1) < 64, fold(c_sum), fold(v_sum))
    x_sums = share(0, me["gx"], partial, line)
    arrive(x_copies)

    def smooth_x(i, carry):
        lo, hi = carry
        s = 3.0 * wx[i + 2] + 2.0 * (wx[i + 1] + wx[i + 3]) + (wx[i] + wx[i + 4])
        wy[i, 8 : 8 + nj, :] = s
        for at in range(2):
            yslo[at, pl.ds(i, 1), :] = s[at : at + 1]
            yshi[at, pl.ds(i, 1), :] = s[nj - 2 + at : nj - 1 + at]
        mine = (lane >> 1) == i
        lo = jnp.where(mine, pltpu.roll(s[:, 0:128], 2 * i, 1), lo)
        hi = jnp.where(mine, pltpu.roll(s[:, nk - 128 : nk], lax.rem(2 * i + 2, 128), 1), hi)
        return lo, hi

    none = jnp.zeros((nj, 128), F32)
    lo, hi = lax.fori_loop(0, ni, smooth_x, (none, none), unroll=4)
    zslo[...] = lo
    zshi[...] = hi
    side_copies = []
    for at, (b, c) in enumerate(SIDE_STEPS):
        if c:
            rows = (slice(nj - 8, nj), slice(0, nj), slice(0, 8))[1 - b]
            to = (slice(0, 8), slice(8, 8 + nj), slice(8 + nj, 16 + nj))[1 - b]
            src = (zslo if c < 0 else zshi).at[rows]
            dst = rzz.at[1 if c < 0 else 0, to]
        else:
            src, dst = (yslo, ryhi) if b < 0 else (yshi, rylo)
        swap(side_copies, src, dst, fsend.at[at], frecv.at[at], (0, b, c))
    all_sums = share(n["gx"], me["gy"] * nz + me["gz"], gather(0, x_sums), sheet)
    arrive(side_copies)

    def smooth_rows(ref, at):
        return (
            3.0 * ref[at, 8 : 8 + nj, :]
            + 2.0 * (ref[at, 7 : 7 + nj, :] + ref[at, 9 : 9 + nj, :])
            + (ref[at, 6 : 6 + nj, :] + ref[at, 10 : 10 + nj, :])
        )

    for side in range(2):
        packs[side] = smooth_rows(rzz, side)

    def smooth_y(i, carry):
        for at in range(2):
            wy[i, 6 + at : 7 + at, :] = rylo[at, pl.ds(i, 1), :]
            wy[i, 8 + nj + at : 9 + nj + at, :] = ryhi[at, pl.ds(i, 1), :]
        out[i] = smooth_rows(wy, i)
        return carry

    lax.fori_loop(0, ni, smooth_y, 0, unroll=4)
    totals[...] = gather(n["gx"], all_sums)
    for copies in (beside, below, far, x_copies, side_copies):
        finish(copies)


def last_pass(cells, field, packs, totals, out, comp, vol):
    ni, nj, nk = field.shape
    both = totals[...]
    first = iota((1, 128), 1) < 64
    comp[0, 0] = jnp.sum(jnp.where(first, both, 0.0)) / cells
    vol[0, 0] = jnp.sum(jnp.where(first, 0.0, both)) / cells
    lanes = iota((nj, nk), 1)

    def twice(x):
        return jnp.concatenate([x, x], 1)

    def smooth_z(i, carry):
        t = field[i]
        left, right = packs[0], packs[1]
        a1 = jnp.where(lanes < 1, twice(pltpu.roll(left, 127 - 2 * i, 1)), pltpu.roll(t, 1, 1))
        a2 = jnp.where(lanes < 2, twice(pltpu.roll(left, lax.rem(128 - 2 * i, 128), 1)), pltpu.roll(t, 2, 1))
        b1 = jnp.where(lanes >= nk - 1, twice(pltpu.roll(right, 127 - 2 * i, 1)), pltpu.roll(t, nk - 1, 1))
        b2 = jnp.where(lanes >= nk - 2, twice(pltpu.roll(right, 126 - 2 * i, 1)), pltpu.roll(t, nk - 2, 1))
        out[i] = 3.0 * t + 2.0 * (a1 + b1) + (a2 + b2)
        return carry

    lax.fori_loop(0, ni, smooth_z, 0, unroll=4)


def on_device(sizes, displacement, density, stiffness):
    ni, nj, nk = density.shape
    vmem = pl.BlockSpec(memory_space=pltpu.VMEM)
    smem = pl.BlockSpec(memory_space=pltpu.SMEM)
    hbm = pl.BlockSpec(memory_space=pltpu.HBM)
    members = sizes[0] + sizes[1] * sizes[2]
    scratch = [
        displacement.shape, density.shape, stiffness.shape,
        (3, nj, nk), (3, ni, nk), (8, nk), (2, 2, nj, 128), (3, ni, nk), (8, nk), (nj, 128),
        (2, 3, ni + 1, nj + 8, nk),
    ]
    later = [
        (ni + 4, nj, nk), (ni, nj + 16, nk),
        (2, ni, nk), (2, ni, nk), (2, ni, nk), (2, ni, nk),
        (nj, 128), (nj, 128), (2, nj + 16, 128), (members, 1, 128),
    ]
    field, packs, totals = pl.pallas_call(
        functools.partial(kernel, sizes),
        out_shape=(
            jax.ShapeDtypeStruct((ni, nj, nk), F32),
            jax.ShapeDtypeStruct((2, nj, 128), F32),
            jax.ShapeDtypeStruct((1, 128), F32),
        ),
        in_specs=[hbm] * 3,
        out_specs=(vmem, vmem, vmem),
        scratch_shapes=[pltpu.VMEM(shape, F32) for shape in scratch]
        + [pltpu.VMEM((nj // 8, (ni + 1) * 128, nk), BF16), pltpu.VMEM((384, 256), BF16)]
        + [pltpu.VMEM(shape, F32) for shape in later]
        + [pltpu.SemaphoreType.DMA((count,)) for count in (3, 7, 7, 10, 10, members, members)],
        compiler_params=pltpu.CompilerParams(
            collective_id=0, has_side_effects=True, vmem_limit_bytes=24 * 1024 * 1024
        ),
    )(*(pltpu.with_memory_space_constraint(x, pltpu.HBM) for x in (displacement, density, stiffness)))
    cells = float(ni * nj * nk * sizes[0] * sizes[1] * sizes[2])
    filtered, comp, vol = pl.pallas_call(
        functools.partial(last_pass, cells),
        out_shape=(
            jax.ShapeDtypeStruct((ni, nj, nk), F32),
            jax.ShapeDtypeStruct((1, 1), F32),
            jax.ShapeDtypeStruct((1, 1), F32),
        ),
        in_specs=[vmem] * 3,
        out_specs=(vmem, smem, smem),
        compiler_params=pltpu.CompilerParams(vmem_limit_bytes=24 * 1024 * 1024),
    )(field, packs, totals)
    return filtered, comp.reshape(()), vol.reshape(())


def solution(mesh):
    sizes = tuple(mesh.shape[axis] for axis in AXES)
    return jax.shard_map(
        functools.partial(on_device, sizes),
        mesh=mesh,
        in_specs=(P(None, "gx", "gy", "gz"), P("gx", "gy", "gz"), P()),
        out_specs=(P("gx", "gy", "gz"), P(), P()),
        check_vma=False,
    )
```

profile of v0, /device:TPU:0, one launch (start us, length us, event | category | flops | bytes accessed | tf_op | source)
XLA Modules:
  0.0 25.6 jit_solution(9167640272630797115)
XLA Ops:
  0.6 23.0 %shard_map.58 = (f32[16,32,256]{2,1,0:T(8,128)S(1)}, f32[2,32,128]{2,1,0:T(8,128)S(1)}, f32[1,128]{1,0:T(1,128)S(1)}) custom-call(f32[3,16,32,256]{3,2,1,0:T(8,128)} %u_hbm.1, f32[16,32,256]{2,1,0:T(8,128)} %rho_hbm.1, f32[24,24]{1,0:T(8,128)} %stiff_hbm.1), custom_call_target="tpu_custom_call" | custom-call | tf_op jit(solution)/shard_map/pallas_call | solution.py:410
  23.6 2.0 %shard_map.59 = (f32[16,32,256]{2,1,0:T(8,128)}, f32[1,1]{1,0:T(1,128)}, f32[1,1]{1,0:T(1,128)}) custom-call(f32[16,32,256]{2,1,0:T(8,128)S(1)} %get-tuple-element.9.field, f32[2,32,128]{2,1,0:T(8,128)S(1)} %get-tuple-element.10.packs, f32[1,128]{1,0:T(1,128)S(1)} %get-tuple-element.11.totals), custom_call_target="tpu_custom_call" | custom-call | tf_op jit(solution)/shard_map/pallas_call | solution.py:428
where the time goes:
time: 25.8 us; the launch traced here: 25.6 us
  Pallas kernels  25 us (97%)
  between operations  0.64 us (2%)
    pallas_call x1, Pallas kernels, on_device(): pl.pallas_call(functools.partial(kernel, sizes), out_shape=(jax.ShapeDtyp...  23 us
    pallas_call x1, Pallas kernels, on_device(): pl.pallas_call(functools.partial(last_pass, cells), out_shape=(jax.ShapeD...  2.02 us

commit v1 on v0

--- a/solution.py
+++ b/solution.py
@@ -31,36 +31,34 @@
 
 
 def band_weights(stiff):
-    rows, cols = 192, 256
+    rows, cols = 192, 128
     pick = jnp.where((iota((rows, 24), 0) >> 3) == iota((rows, 24), 1), 1.0, 0.0).astype(F32)
 
     def column(shape):
         col = iota(shape, 1)
-        a, g, s = col >> 7, (col >> 4) & 7, col & 7
-        cm = jnp.where(g == 6, s, g)
-        c = jnp.where(cm >= 3, 1, 0)
-        m = cm - 3 * c
-        valid = (g < 6) | ((g == 6) & (s < 6))
-        return 8 * m + 4 * a + c, valid, jnp.where(g == 6, 8, s), (col >> 3) & 1
+        a, m, s = col >> 6, (col >> 4) & 3, col & 15
+        edge = m == 3
+        c = jnp.where(edge, jnp.where(s >= 3, 1, 0), s >> 3)
+        m = jnp.where(edge, s - 3 * c, m)
+        valid = jnp.logical_not(edge) | (s < 6)
+        return 8 * m + 4 * a + c, valid, jnp.where(edge, 8, s & 7)
 
     total = None
     for b in (0, 1):
-        q, valid, _, _ = column((24, cols))
+        q, valid, _ = column((24, cols))
         place = jnp.where((iota((24, cols), 0) == q + 2 * b) & valid, 1.0, 0.0).astype(F32)
         wide = jnp.dot(stiff, place, precision=lax.Precision.HIGHEST, preferred_element_type=F32)
         tall = jnp.dot(pick, wide, precision=lax.Precision.HIGHEST, preferred_element_type=F32)
-        _, _, jj, _ = column((rows, cols))
+        _, _, jj = column((rows, cols))
         term = jnp.where(jj - (iota((rows, cols), 0) & 7) == b, tall, 0.0)
         total = term if total is None else total + term
-    high = total.astype(BF16).astype(F32)
-    _, _, _, lo_col = column((rows, cols))
-    low = jnp.where(lo_col == 0, total - high, 0.0)
-    return high.astype(BF16), low.astype(BF16)
+    high = total.astype(BF16)
+    return jnp.concatenate([high, (total - high.astype(F32)).astype(BF16)], 1)
 
 
 def kernel(
     sizes, u_hbm, rho_hbm, stiff_hbm, out, packs, totals,
-    u, rho, stiff, rx, ry, rxy, rz, ys, yd, zs, field, parts, weights, wx, wy,
+    u, rho, stiff, rx, ry, rxy, rz, ys, yd, zs, field, edge, line_f, line_u, parts, weights, wx, wy,
     yslo, yshi, rylo, ryhi, zslo, zshi, rzz, sums, insem, nsend, nrecv, fsend, frecv, gsend, grecv,
 ):
     ni, nj, nk = rho.shape
@@ -156,13 +154,11 @@
     node_swap((1, 0, 0))
     loads[1].wait()
     lane = iota((nj, 128), 1)
-    def pack(i, acc):
-        for m in range(3):
-            at = m * ni + i
-            acc = jnp.where(lane == at, pltpu.roll(u[m, i, :, 0:128], at, 1), acc)
-        return acc
-
-    zs[...] = lax.fori_loop(0, ni, pack, jnp.zeros((nj, 128), F32), unroll=4)
+    packed = jnp.zeros((nj, 128), F32)
+    for at in range(3 * ni):
+        column = u[at // ni, at % ni, :, 0:128]
+        packed = jnp.where(lane == at, pltpu.roll(column, at, 1) if at else column, packed)
+    zs[...] = packed
     for step in NODE_STEPS:
         if step[2]:
             node_swap(step)
@@ -174,98 +170,91 @@
     node_swap((0, 1, 0))
     node_swap((1, 1, 0))
     loads[0].wait()
-    high, low = band_weights(stiff[...])
-    weights[0:192, :] = high
-    weights[192:384, :] = low
+    weights[...] = band_weights(stiff[...])
 
     last = iota((nj, nk), 1) == nk - 1
-    last8 = iota((8, nk), 1) == nk - 1
-    sub8 = iota((8, nk), 0)
-
-    def split(f):
-        hi = f.astype(BF16).astype(F32)
-        return jnp.concatenate([hi, f - hi], 0).astype(BF16)
-
-    def put(jt, to, at, f):
-        parts[jt, pl.ds(pl.multiple_of(to * 128, 128) + at, 16), :] = split(f)
-
-    def first_half(m, to, base):
-        field[0, m, to, 0:nj, :] = base
+    last1 = iota((1, nk), 1) == nk - 1
+    edge[...] = jnp.zeros(edge.shape, F32)
+
+    def beyond(base, col, at, rim):
+        side = pltpu.roll(col, 127 - at, 1)
+        return jnp.where(rim, jnp.concatenate([side, side], 1), pltpu.roll(base, nk - 1, 1))
+
+    def sharp(x):
+        return x + (x - x.astype(BF16).astype(F32))
+
+    def layer(m, to, base, moved):
+        for c, x in enumerate((base, moved)):
+            f = sharp(x)
+            for h in range(2):
+                field[c, m, to, h, 0:nj, :] = f[:, 128 * h : 128 * h + 128]
+            for jt in range(1, nj // 8):
+                edge[to, jt - 1, 3 * c + m : 3 * c + m + 1, :] = x[8 * jt : 8 * jt + 1, :]
         for jt in range(nj // 8):
-            put(jt, to, 16 * m, base[8 * jt : 8 * jt + 8])
-
-    def second_half(m, to, base, col, at):
-        side = pltpu.roll(col, 127 - at, 1)
-        moved = jnp.where(last, jnp.concatenate([side, side], 1), pltpu.roll(base, nk - 1, 1))
-        field[1, m, to, 0:nj, :] = moved
-        for jt in range(nj // 8):
-            put(jt, to, 48 + 16 * m, moved[8 * jt : 8 * jt + 8])
-
-    def next_row(m, to, row, corner, at):
-        row8 = jnp.broadcast_to(row, (8, nk))
-        field[0, m, to, nj : nj + 8, :] = row8
-        side8 = pltpu.roll(corner, 127 - at, 1)
-        field[1, m, to, nj : nj + 8, :] = jnp.where(
-            last8, jnp.concatenate([side8, side8], 1), pltpu.roll(row8, nk - 1, 1)
-        )
-
-    def edges(to):
-        for jt in range(nj // 8):
-            edge = jnp.zeros((8, nk), F32)
-            for cm in range(6):
-                c, m = divmod(cm, 3)
-                row = field[c, m, to, 8 * jt + 8 : 8 * jt + 9, :]
-                edge = jnp.where(sub8 == cm, jnp.broadcast_to(row, (8, nk)), edge)
-            put(jt, to, 96, edge)
-
-    def own_first(i, carry):
+            rows = slice(8 * jt, 8 * jt + 8)
+            parts[jt, to, 16 * m : 16 * m + 16, :] = jnp.concatenate([base[rows], moved[rows]], 0).astype(BF16)
+
+    def next_row(c, m, to, x, f):
+        for h in range(2):
+            field[c, m, to, h, nj : nj + 1, :] = f[:, 128 * h : 128 * h + 128]
+        edge[to, nj // 8 - 1, 3 * c + m : 3 * c + m + 1, :] = x
+
+    def own_layer(i, carry):
         for m in range(3):
-            first_half(m, i, u[m, i])
-        for jt in range(nj // 8):
-            parts[jt, pl.ds(pl.multiple_of(i * 128, 128) + 112, 16), :] = jnp.zeros((16, nk), BF16)
+            base = u[m, i]
+            layer(m, i, base, beyond(base, rz[0, 0], m * ni + i, last))
         return carry
 
-    def own_second(i, carry):
-        for m in range(3):
-            second_half(m, i, u[m, i], rz[0, 0], m * ni + i)
+    def own_row(i, carry):
+        for c in range(2):
+            for m in range(3):
+                at = pl.ds(i, 1)
+                next_row(c, m, i, line_u[3 * c + m, at, :], line_f[3 * c + m, at, :])
         return carry
 
-    def own_edges(i, carry):
-        for m in range(3):
-            next_row(m, i, ry[m, pl.ds(i, 1), :], rz[0, 1, 0:8, :], m * ni + i)
-        edges(i)
-        return carry
-
-    lax.fori_loop(0, ni, own_first, 0)
-    for jt in range(nj // 8):
-        parts[jt, ni * 128 + 112 : ni * 128 + 128, :] = jnp.zeros((16, nk), BF16)
     loads[2].wait()
     wy[0, 0:nj, :] = 1.0 / (
         line_sum(me["gy"] * nj + iota((nj, nk), 0), ny * nj)
         * line_sum(me["gz"] * nk + iota((nj, nk), 1), nz * nk)
     )
     arrive(beside)
-    lax.fori_loop(0, ni, own_second, 0, unroll=2)
+    lax.fori_loop(0, ni, own_layer, 0, unroll=2)
     arrive(below)
-    lax.fori_loop(0, ni, own_edges, 0, unroll=2)
+    for m in range(3):
+        base = ry[m]
+        mine = iota((ni, 128), 1) == iota((ni, 128), 0) + m * ni
+        corner = jnp.sum(jnp.where(mine, rz[0, 1, 0:1, :], 0.0), axis=1, keepdims=True)
+        moved = jnp.where(iota((ni, nk), 1) == nk - 1, corner, pltpu.roll(base, nk - 1, 1))
+        for c, x in enumerate((base, moved)):
+            line_u[3 * c + m] = x
+            line_f[3 * c + m] = sharp(x)
+    lax.fori_loop(0, ni, own_row, 0, unroll=4)
     arrive(far)
     for m in range(3):
-        first_half(m, ni, rx[m])
-        second_half(m, ni, rx[m], rz[1, 0], m * ni)
-        next_row(m, ni, rxy[m : m + 1, :], rz[1, 1, 0:8, :], m * ni)
-    edges(ni)
+        base = rx[m]
+        layer(m, ni, base, beyond(base, rz[1, 0], m * ni, last))
+        row = rxy[m : m + 1, :]
+        moved = beyond(row, rz[1, 1, 0:1, :], m * ni, last1)
+        for c, x in enumerate((row, moved)):
+            next_row(c, m, ni, x, sharp(x))
+
+    none8 = jnp.zeros((8, nk), F32)
+
+    def tile(jt, p):
+        return [parts[jt, p], jnp.concatenate([edge[p, jt], none8], 0).astype(BF16)]
 
     def plane(i, carry):
         c_sum, v_sum = carry
         inv_x = 1.0 / line_sum(jnp.full((8, nk), me["gx"] * ni + i, jnp.int32), n["gx"] * ni)
         for jt in range(nj // 8):
-            data = parts[jt, pl.ds(pl.multiple_of(i * 128, 128), 256), :]
-            product = jnp.dot(weights[...], data, preferred_element_type=F32)
+            data = tile(jt, i) + tile(jt, i + 1)
+            product = jnp.dot(weights[...], jnp.concatenate(data + data, 0), preferred_element_type=F32)
             energy = None
             for r in range(24):
                 m, a, b, c = r >> 3, (r >> 2) & 1, (r >> 1) & 1, r & 1
-                v = product[8 * r : 8 * r + 8] + product[192 + 8 * r : 200 + 8 * r]
-                term = v * field[c, m, i + a, 8 * jt + b : 8 * jt + b + 8, :]
+                rows = pl.ds(8 * jt + b, 8)
+                f = [field[c, m, i + a, h, rows, :] for h in range(2)]
+                term = product[8 * r : 8 * r + 8] * jnp.concatenate(f, 1)
                 energy = term if energy is None else energy + term
             d = rho[i, 8 * jt : 8 * jt + 8, :]
             c_sum = c_sum + (VOID + d * d * d * (1.0 - VOID)) * energy
@@ -374,21 +363,24 @@
     comp[0, 0] = jnp.sum(jnp.where(first, both, 0.0)) / cells
     vol[0, 0] = jnp.sum(jnp.where(first, 0.0, both)) / cells
     lanes = iota((nj, nk), 1)
+    even = lax.rem(iota((nj, 128), 1), 2) == 0
+    left, right = packs[0], packs[1]
+    left = jnp.where(even, left + 2.0 * pltpu.roll(left, 127, 1), left)
+    right = jnp.where(even, right, right + 2.0 * pltpu.roll(right, 1, 1))
+    apart = jnp.abs(iota((nk, nk), 0) - iota((nk, nk), 1))
+    band = jnp.maximum(3 - apart, 0).astype(F32).astype(BF16)
 
     def twice(x):
         return jnp.concatenate([x, x], 1)
 
-    def smooth_z(i, carry):
+    for i in range(ni):
         t = field[i]
-        left, right = packs[0], packs[1]
-        a1 = jnp.where(lanes < 1, twice(pltpu.roll(left, 127 - 2 * i, 1)), pltpu.roll(t, 1, 1))
-        a2 = jnp.where(lanes < 2, twice(pltpu.roll(left, lax.rem(128 - 2 * i, 128), 1)), pltpu.roll(t, 2, 1))
-        b1 = jnp.where(lanes >= nk - 1, twice(pltpu.roll(right, 127 - 2 * i, 1)), pltpu.roll(t, nk - 1, 1))
-        b2 = jnp.where(lanes >= nk - 2, twice(pltpu.roll(right, 126 - 2 * i, 1)), pltpu.roll(t, nk - 2, 1))
-        out[i] = 3.0 * t + 2.0 * (a1 + b1) + (a2 + b2)
-        return carry
-
-    lax.fori_loop(0, ni, smooth_z, 0, unroll=4)
+        high = t.astype(BF16)
+        low = (t - high.astype(F32)).astype(BF16)
+        own = jnp.dot(high, band, preferred_element_type=F32) + jnp.dot(low, band, preferred_element_type=F32)
+        lo = twice(pltpu.roll(left, (128 - 2 * i) % 128, 1))
+        hi = twice(pltpu.roll(right, 126 - 2 * i, 1))
+        out[i] = own + jnp.where(lanes < 2, lo, jnp.where(lanes >= nk - 2, hi, 0.0))
 
 
 def on_device(sizes, displacement, density, stiffness):
@@ -400,7 +392,7 @@
     scratch = [
         displacement.shape, density.shape, stiffness.shape,
         (3, nj, nk), (3, ni, nk), (8, nk), (2, 2, nj, 128), (3, ni, nk), (8, nk), (nj, 128),
-        (2, 3, ni + 1, nj + 8, nk),
+        (2, 3, ni + 1, 2, nj + 8, 128), (ni + 1, nj // 8, 8, nk), (6, ni, nk), (6, ni, nk),
     ]
     later = [
         (ni + 4, nj, nk), (ni, nj + 16, nk),
@@ -417,7 +409,7 @@
         in_specs=[hbm] * 3,
         out_specs=(vmem, vmem, vmem),
         scratch_shapes=[pltpu.VMEM(shape, F32) for shape in scratch]
-        + [pltpu.VMEM((nj // 8, (ni + 1) * 128, nk), BF16), pltpu.VMEM((384, 256), BF16)]
+        + [pltpu.VMEM((nj // 8, ni + 1, 48, nk), BF16), pltpu.VMEM((192, 256), BF16)]
         + [pltpu.VMEM(shape, F32) for shape in later]
         + [pltpu.SemaphoreType.DMA((count,)) for count in (3, 7, 7, 10, 10, members, members)],
         compiler_params=pltpu.CompilerParams(

time: 25.8 us -> 23.3 us (0.903)
  Pallas kernels: 25 us -> 22.5 us
    pallas_call x1, Pallas kernels: 23 us -> 20.9 us  [on_device(): pl.pallas_call(functools.partial(kernel, sizes), out_shape=(jax.ShapeDtyp...]
    pallas_call x1, Pallas kernels: 2.02 us -> 1.66 us  [on_device(): pl.pallas_call(functools.partial(last_pass, cells), out_shape=(jax.ShapeD...]
where the time goes in v1:
time: 23.3 us; the launch traced here: 23.2 us
  Pallas kernels  22.5 us (97%)
  between operations  0.64 us (3%)
    pallas_call x1, Pallas kernels, on_device(): pl.pallas_call(functools.partial(kernel, sizes), out_shape=(jax.ShapeDtyp...  20.9 us
    pallas_call x1, Pallas kernels, on_device(): pl.pallas_call(functools.partial(last_pass, cells), out_shape=(jax.ShapeD...  1.66 us

profile of v1, /device:TPU:0, one launch (start us, length us, event | category | flops | bytes accessed | tf_op | source)
XLA Modules:
  0.0 23.2 jit_solution(16691739059030463034)
XLA Ops:
  0.6 20.9 %shard_map.58 = (f32[16,32,256]{2,1,0:T(8,128)S(1)}, f32[2,32,128]{2,1,0:T(8,128)S(1)}, f32[1,128]{1,0:T(1,128)S(1)}) custom-call(f32[3,16,32,256]{3,2,1,0:T(8,128)} %u_hbm.1, f32[16,32,256]{2,1,0:T(8,128)} %rho_hbm.1, f32[24,24]{1,0:T(8,128)} %stiff_hbm.1), custom_call_target="tpu_custom_call" | custom-call | tf_op jit(solution)/shard_map/pallas_call | solution.py:402
  21.5 1.7 %shard_map.59 = (f32[16,32,256]{2,1,0:T(8,128)}, f32[1,1]{1,0:T(1,128)}, f32[1,1]{1,0:T(1,128)}) custom-call(f32[16,32,256]{2,1,0:T(8,128)S(1)} %get-tuple-element.9.field, f32[2,32,128]{2,1,0:T(8,128)S(1)} %get-tuple-element.10.packs, f32[1,128]{1,0:T(1,128)S(1)} %get-tuple-element.11.totals), custom_call_target="tpu_custom_call" | custom-call | tf_op jit(solution)/shard_map/pallas_call | solution.py:420

commit v2 on v1

--- a/solution.py
+++ b/solution.py
@@ -58,7 +58,7 @@
 
 def kernel(
     sizes, u_hbm, rho_hbm, stiff_hbm, out, packs, totals,
-    u, rho, stiff, rx, ry, rxy, rz, ys, yd, zs, field, edge, line_f, line_u, parts, weights, wx, wy,
+    u, rho, stiff, rx, ry, rxy, rz, ys, yd, zs, field, edge, line_f, line_u, inv, parts, weights, wx, wy,
     yslo, yshi, rylo, ryhi, zslo, zshi, rzz, sums, insem, nsend, nrecv, fsend, frecv, gsend, grecv,
 ):
     ni, nj, nk = rho.shape
@@ -172,38 +172,39 @@
     loads[0].wait()
     weights[...] = band_weights(stiff[...])
 
-    last = iota((nj, nk), 1) == nk - 1
-    last1 = iota((1, nk), 1) == nk - 1
+    last = iota((nj, 128), 1) == 127
     edge[...] = jnp.zeros(edge.shape, F32)
-
-    def beyond(base, col, at, rim):
-        side = pltpu.roll(col, 127 - at, 1)
-        return jnp.where(rim, jnp.concatenate([side, side], 1), pltpu.roll(base, nk - 1, 1))
+    nq = nj // 16
 
     def sharp(x):
         return x + (x - x.astype(BF16).astype(F32))
 
-    def layer(m, to, base, moved):
-        for c, x in enumerate((base, moved)):
-            f = sharp(x)
-            for h in range(2):
-                field[c, m, to, h, 0:nj, :] = f[:, 128 * h : 128 * h + 128]
-            for jt in range(1, nj // 8):
-                edge[to, jt - 1, 3 * c + m : 3 * c + m + 1, :] = x[8 * jt : 8 * jt + 1, :]
-        for jt in range(nj // 8):
-            rows = slice(8 * jt, 8 * jt + 8)
-            parts[jt, to, 16 * m : 16 * m + 16, :] = jnp.concatenate([base[rows], moved[rows]], 0).astype(BF16)
+    def pair(x, q):
+        return jnp.concatenate([x[16 * q : 16 * q + 8], x[16 * q + 8 : 16 * q + 16]], 1)
+
+    def layer(h, to, at, source, col):
+        for m in range(3):
+            x = source(m, h)
+            side = source(m, 1) if h == 0 else col
+            turn = 127 if h == 0 else 127 - (m * ni + at)
+            moved = jnp.where(last, pltpu.roll(side, turn, 1), pltpu.roll(x, 127, 1))
+            for c, y in enumerate((x, moved)):
+                field[c, m, to, h, 0:nj, :] = sharp(y)
+                for jt in range(nj // 8 - 1):
+                    edge[h, jt // 2, to, 3 * c + m : 3 * c + m + 1, 128 * (jt % 2) : 128 * (jt % 2) + 128] = (
+                        y[8 * jt + 8 : 8 * jt + 9, :]
+                    )
+            for q in range(nq):
+                parts[h, q, to, 16 * m : 16 * m + 16, :] = jnp.concatenate([pair(x, q), pair(moved, q)], 0).astype(BF16)
+
+    def own(i):
+        return lambda m, h: u[m, i, :, 128 * h : 128 * h + 128]
 
     def next_row(c, m, to, x, f):
         for h in range(2):
-            field[c, m, to, h, nj : nj + 1, :] = f[:, 128 * h : 128 * h + 128]
-        edge[to, nj // 8 - 1, 3 * c + m : 3 * c + m + 1, :] = x
-
-    def own_layer(i, carry):
-        for m in range(3):
-            base = u[m, i]
-            layer(m, i, base, beyond(base, rz[0, 0], m * ni + i, last))
-        return carry
+            half = slice(128 * h, 128 * h + 128)
+            field[c, m, to, h, nj : nj + 1, :] = f[:, half]
+            edge[h, nq - 1, to, 3 * c + m : 3 * c + m + 1, 128:256] = x[:, half]
 
     def own_row(i, carry):
         for c in range(2):
@@ -212,13 +213,48 @@
                 next_row(c, m, i, line_u[3 * c + m, at, :], line_f[3 * c + m, at, :])
         return carry
 
+    none8 = jnp.zeros((8, nk), F32)
+
+    def tile(h, q, p):
+        return [parts[h, q, p], jnp.concatenate([edge[h, q, p], none8], 0).astype(BF16)]
+
+    def unit(i, q, h, c_sum, v_sum):
+        half = slice(128 * h, 128 * h + 128)
+        rows = [slice(16 * q + 8 * t, 16 * q + 8 * t + 8) for t in range(2)]
+        data = tile(h, q, i) + tile(h, q, i + 1)
+        product = jnp.dot(weights[...], jnp.concatenate(data + data, 0), preferred_element_type=F32)
+        energy = None
+        for r in range(24):
+            m, a, b, c = r >> 3, (r >> 2) & 1, (r >> 1) & 1, r & 1
+            f = [field[c, m, i + a, h, 16 * q + 8 * t + b : 16 * q + 8 * t + b + 8, :] for t in range(2)]
+            term = product[8 * r : 8 * r + 8] * jnp.concatenate(f, 1)
+            energy = term if energy is None else energy + term
+        d = jnp.concatenate([rho[i, rows[t], half] for t in range(2)], 1)
+        scale = jnp.concatenate([inv[rows[t], half] for t in range(2)], 1)
+        inv_x = 1.0 / line_sum(jnp.full((8, nk), me["gx"] * ni + i, jnp.int32), n["gx"] * ni)
+        w = (-3.0 * (1.0 - VOID)) * d * d * energy * (inv_x * scale)
+        for t in range(2):
+            wx[i + 2, rows[t], half] = w[:, 128 * t : 128 * t + 128]
+        return c_sum + (VOID + d * d * d * (1.0 - VOID)) * energy, v_sum + d
+
+    def sweep(h):
+        def body(i, carry):
+            layer(h, i + 1, i + 1, own(i + 1), rz[0, 0])
+            return unit(i, 0, h, *carry)
+
+        return body
+
     loads[2].wait()
-    wy[0, 0:nj, :] = 1.0 / (
+    inv[...] = 1.0 / (
         line_sum(me["gy"] * nj + iota((nj, nk), 0), ny * nj)
         * line_sum(me["gz"] * nk + iota((nj, nk), 1), nz * nk)
     )
+    carry = (none8, none8)
+    layer(0, 0, 0, own(0), None)
+    carry = lax.fori_loop(0, ni - 1, sweep(0), carry, unroll=5)
     arrive(beside)
-    lax.fori_loop(0, ni, own_layer, 0, unroll=2)
+    layer(1, 0, 0, own(0), rz[0, 0])
+    carry = lax.fori_loop(0, ni - 1, sweep(1), carry, unroll=5)
     arrive(below)
     for m in range(3):
         base = ry[m]
@@ -229,49 +265,32 @@
             line_u[3 * c + m] = x
             line_f[3 * c + m] = sharp(x)
     lax.fori_loop(0, ni, own_row, 0, unroll=4)
+
+    def upper(i, carry):
+        for q in range(1, nq):
+            for h in range(2):
+                carry = unit(i, q, h, *carry)
+        return carry
+
+    carry = lax.fori_loop(0, ni - 1, upper, carry, unroll=5)
+    x_copies = []
+    swap(x_copies, wx.at[2:4], wx.at[ni + 2 : ni + 4], fsend.at[8], frecv.at[8], (-1, 0, 0))
     arrive(far)
+    for h in range(2):
+        layer(h, ni, 0, lambda m, h: rx[m, :, 128 * h : 128 * h + 128], rz[1, 0])
     for m in range(3):
-        base = rx[m]
-        layer(m, ni, base, beyond(base, rz[1, 0], m * ni, last))
         row = rxy[m : m + 1, :]
-        moved = beyond(row, rz[1, 1, 0:1, :], m * ni, last1)
+        side = pltpu.roll(rz[1, 1, 0:1, :], 127 - m * ni, 1)
+        moved = jnp.where(
+            iota((1, nk), 1) == nk - 1, jnp.concatenate([side, side], 1), pltpu.roll(row, nk - 1, 1)
+        )
         for c, x in enumerate((row, moved)):
             next_row(c, m, ni, x, sharp(x))
-
-    none8 = jnp.zeros((8, nk), F32)
-
-    def tile(jt, p):
-        return [parts[jt, p], jnp.concatenate([edge[p, jt], none8], 0).astype(BF16)]
-
-    def plane(i, carry):
-        c_sum, v_sum = carry
-        inv_x = 1.0 / line_sum(jnp.full((8, nk), me["gx"] * ni + i, jnp.int32), n["gx"] * ni)
-        for jt in range(nj // 8):
-            data = tile(jt, i) + tile(jt, i + 1)
-            product = jnp.dot(weights[...], jnp.concatenate(data + data, 0), preferred_element_type=F32)
-            energy = None
-            for r in range(24):
-                m, a, b, c = r >> 3, (r >> 2) & 1, (r >> 1) & 1, r & 1
-                rows = pl.ds(8 * jt + b, 8)
-                f = [field[c, m, i + a, h, rows, :] for h in range(2)]
-                term = product[8 * r : 8 * r + 8] * jnp.concatenate(f, 1)
-                energy = term if energy is None else energy + term
-            d = rho[i, 8 * jt : 8 * jt + 8, :]
-            c_sum = c_sum + (VOID + d * d * d * (1.0 - VOID)) * energy
-            v_sum = v_sum + d
-            wx[i + 2, 8 * jt : 8 * jt + 8, :] = (
-                (-3.0 * (1.0 - VOID)) * d * d * energy * (inv_x * wy[0, 8 * jt : 8 * jt + 8, :])
-            )
-        return c_sum, v_sum
-
-    zero = jnp.zeros((8, nk), F32)
-    carry = lax.fori_loop(
-        0, 4, lambda t, s: plane(jnp.where(t < 2, t, ni - 4 + t), s), (zero, zero)
-    )
-    x_copies = []
-    swap(x_copies, wx.at[2:4], wx.at[ni + 2 : ni + 4], fsend.at[8], frecv.at[8], (-1, 0, 0))
+    for q in range(nq):
+        for h in range(2):
+            carry = unit(ni - 1, q, h, *carry)
+    c_sum, v_sum = carry
     swap(x_copies, wx.at[ni : ni + 2], wx.at[0:2], fsend.at[9], frecv.at[9], (1, 0, 0))
-    c_sum, v_sum = lax.fori_loop(4, ni, lambda t, s: plane(t - 2, s), carry)
 
     def share(base, mine, value, group):
         sums[base + mine] = value
@@ -392,7 +411,7 @@
     scratch = [
         displacement.shape, density.shape, stiffness.shape,
         (3, nj, nk), (3, ni, nk), (8, nk), (2, 2, nj, 128), (3, ni, nk), (8, nk), (nj, 128),
-        (2, 3, ni + 1, 2, nj + 8, 128), (ni + 1, nj // 8, 8, nk), (6, ni, nk), (6, ni, nk),
+        (2, 3, ni + 1, 2, nj + 8, 128), (2, nj // 16, ni + 1, 8, nk), (6, ni, nk), (6, ni, nk), (nj, nk),
     ]
     later = [
         (ni + 4, nj, nk), (ni, nj + 16, nk),
@@ -409,7 +428,7 @@
         in_specs=[hbm] * 3,
         out_specs=(vmem, vmem, vmem),
         scratch_shapes=[pltpu.VMEM(shape, F32) for shape in scratch]
-        + [pltpu.VMEM((nj // 8, ni + 1, 48, nk), BF16), pltpu.VMEM((192, 256), BF16)]
+        + [pltpu.VMEM((2, nj // 16, ni + 1, 48, nk), BF16), pltpu.VMEM((192, 256), BF16)]
         + [pltpu.VMEM(shape, F32) for shape in later]
         + [pltpu.SemaphoreType.DMA((count,)) for count in (3, 7, 7, 10, 10, members, members)],
         compiler_params=pltpu.CompilerParams(

time: 23.3 us -> 20.8 us (0.89)
  Pallas kernels: 22.5 us -> 20 us
    pallas_call x1, Pallas kernels: 20.9 us -> 18.3 us  [on_device(): pl.pallas_call(functools.partial(kernel, sizes), out_shape=(jax.ShapeDtyp...]
where the time goes in v2:
time: 20.8 us; the launch traced here: 20.6 us
  Pallas kernels  20 us (96%)
  between operations  0.64 us (3%)
    pallas_call x1, Pallas kernels, on_device(): pl.pallas_call(functools.partial(kernel, sizes), out_shape=(jax.ShapeDtyp...  18.3 us
    pallas_call x1, Pallas kernels, on_device(): pl.pallas_call(functools.partial(last_pass, cells), out_shape=(jax.ShapeD...  1.66 us

profile of v2, /device:TPU:0, one launch (start us, length us, event | category | flops | bytes accessed | tf_op | source)
XLA Modules:
  0.0 20.6 jit_solution(2404268066393467114)
XLA Ops:
  0.6 18.3 %shard_map.58 = (f32[16,32,256]{2,1,0:T(8,128)S(1)}, f32[2,32,128]{2,1,0:T(8,128)S(1)}, f32[1,128]{1,0:T(1,128)S(1)}) custom-call(f32[3,16,32,256]{3,2,1,0:T(8,128)} %u_hbm.1, f32[16,32,256]{2,1,0:T(8,128)} %rho_hbm.1, f32[24,24]{1,0:T(8,128)} %stiff_hbm.1), custom_call_target="tpu_custom_call" | custom-call | tf_op jit(solution)/shard_map/pallas_call | solution.py:421
  19.0 1.7 %shard_map.59 = (f32[16,32,256]{2,1,0:T(8,128)}, f32[1,1]{1,0:T(1,128)}, f32[1,1]{1,0:T(1,128)}) custom-call(f32[16,32,256]{2,1,0:T(8,128)S(1)} %get-tuple-element.9.field, f32[2,32,128]{2,1,0:T(8,128)S(1)} %get-tuple-element.10.packs, f32[1,128]{1,0:T(1,128)S(1)} %get-tuple-element.11.totals), custom_call_target="tpu_custom_call" | custom-call | tf_op jit(solution)/shard_map/pallas_call | solution.py:439

commit v3 on v2

--- a/solution.py
+++ b/solution.py
@@ -14,7 +14,7 @@
 F32 = jnp.float32
 BF16 = jnp.bfloat16
 NODE_STEPS = [(a, b, c) for a in (0, 1) for b in (0, 1) for c in (0, 1) if a + b + c]
-SIDE_STEPS = [(b, c) for b in (-1, 0, 1) for c in (-1, 0, 1) if b or c]
+AROUND = [(a, b, c) for a in (-1, 0, 1) for b in (-1, 0, 1) for c in (-1, 0, 1) if a or b or c]
 
 
 def iota(shape, dim):
@@ -57,9 +57,11 @@
 
 
 def kernel(
-    sizes, u_hbm, rho_hbm, stiff_hbm, out, packs, totals,
-    u, rho, stiff, rx, ry, rxy, rz, ys, yd, zs, field, edge, line_f, line_u, inv, parts, weights, wx, wy,
-    yslo, yshi, rylo, ryhi, zslo, zshi, rzz, sums, insem, nsend, nrecv, fsend, frecv, gsend, grecv,
+    sizes, u_hbm, rho_hbm, stiff_hbm, out, totals,
+    u, rho, stiff, rx, ry, rxy, rz, ys, yd, zs,
+    field, edge, line_f, line_u, inv, parts, weights, band, wx, wy,
+    ysend, corner_send, zsend, rows_in, corner_in, rzz, rzs, yrow,
+    sums, insem, nsend, nrecv, fsend, frecv, gsend, grecv,
 ):
     ni, nj, nk = rho.shape
     n = dict(zip(AXES, sizes))
@@ -95,15 +97,49 @@
     for ids in line + sheet:
         pl.semaphore_signal(barrier, inc=1, device_id=ids, device_id_type=MESH)
     peers = len(line) + len(sheet)
+    for step in AROUND:
+        if step[0] and (step[1] or step[2]):
+            ids, ok = hop(step)
+            peers = peers + jnp.where(ok, 1, 0)
+
+            @pl.when(ok)
+            def _():
+                pl.semaphore_signal(barrier, inc=1, device_id=ids, device_id_type=MESH)
+
+    def node_route(step):
+        a, b, c = step
+        if c:
+            return (zs.at[0:8], rz.at[a, b, 0:8]) if b else (zs, rz.at[a, b])
+        if b:
+            return (yd, rxy) if a else (ys, ry)
+        return u_hbm.at[:, 0], rx
+
+    def face_route(step):
+        a, b, c = step
+        hi_a, hi_b, hi_c = a > 0, b > 0, c > 0
+        if c:
+            rows = (slice(nj - 8, nj), slice(0, nj), slice(0, 8))[1 - b]
+            to = (slice(0, 8), slice(8, 8 + nj), slice(8 + nj, 16 + nj))[1 - b]
+            return zsend.at[int(hi_c), rows], rzz.at[1 - hi_c, 1 - a, to]
+        if a and b:
+            return corner_send.at[int(hi_a), int(hi_b)], corner_in.at[1 - hi_a, 1 - hi_b]
+        if b:
+            at = 2 * (1 - hi_b)
+            return ysend.at[int(hi_b)], rows_in.at[at : at + 2, 8 : 8 + ni]
+        return (wx.at[ni : ni + 2], wx.at[0:2]) if hi_a else (wx.at[2:4], wx.at[ni + 2 : ni + 4])
+
+    def clear(dst, step):
+        @pl.when(jnp.logical_not(hop(step)[1]))
+        def _():
+            dst[...] = jnp.zeros(dst.shape, F32)
+
     for step in NODE_STEPS:
-        if step[0] and sum(step) > 1:
-            for way in (step, minus(step)):
-                ids, ok = hop(way)
-                peers = peers + jnp.where(ok, 1, 0)
-
-                @pl.when(ok)
-                def _():
-                    pl.semaphore_signal(barrier, inc=1, device_id=ids, device_id_type=MESH)
+        clear(node_route(step)[1], step)
+    for step in AROUND:
+        clear(face_route(step)[1], minus(step))
+    apart = jnp.abs(iota((nk, nk), 0) - iota((nk, nk), 1))
+    band[...] = jnp.maximum(3 - apart, 0).astype(F32).astype(BF16)
+    edge[...] = jnp.zeros(edge.shape, F32)
 
     pl.semaphore_wait(barrier, peers)
 
@@ -113,25 +149,21 @@
             src_ref=src, dst_ref=dst, send_sem=send_sem, recv_sem=recv_sem,
             device_id=ids, device_id_type=MESH,
         )
-        copies.append((copy, sends, hop(minus(step))[1], dst))
+        copies.append((copy, sends, hop(minus(step))[1]))
 
         @pl.when(sends)
         def _():
             copy.start()
 
     def arrive(copies):
-        for copy, _, takes, dst in copies:
+        for copy, _, takes in copies:
 
             @pl.when(takes)
             def _():
                 copy.wait_recv()
 
-            @pl.when(jnp.logical_not(takes))
-            def _():
-                dst[...] = jnp.zeros(dst.shape, F32)
-
     def finish(copies):
-        for copy, sends, _, _ in copies:
+        for copy, sends, _ in copies:
 
             @pl.when(sends)
             def _():
@@ -142,16 +174,18 @@
     def node_swap(step):
         a, b, c = step
         at = NODE_STEPS.index(step)
-        if c:
-            src, dst = (zs.at[0:8], rz.at[a, b, 0:8]) if b else (zs, rz.at[a, b])
-        elif b:
-            src, dst = (yd, rxy) if a else (ys, ry)
-        else:
-            src, dst = u_hbm.at[:, 0], rx
+        src, dst = node_route(step)
         copies = far if a else (below if b else beside)
         swap(copies, src, dst, nsend.at[at], nrecv.at[at], minus(step))
 
+    def face_swap(copies, step):
+        at = AROUND.index(step)
+        src, dst = face_route(step)
+        swap(copies, src, dst, fsend.at[at], frecv.at[at], step)
+
     node_swap((1, 0, 0))
+    loads[0].wait()
+    weights[...] = band_weights(stiff[...])
     loads[1].wait()
     lane = iota((nj, 128), 1)
     packed = jnp.zeros((nj, 128), F32)
@@ -169,11 +203,8 @@
         yd[m : m + 1, :] = u[m, 0, 0:1, :]
     node_swap((0, 1, 0))
     node_swap((1, 1, 0))
-    loads[0].wait()
-    weights[...] = band_weights(stiff[...])
 
     last = iota((nj, 128), 1) == 127
-    edge[...] = jnp.zeros(edge.shape, F32)
     nq = nj // 16
 
     def sharp(x):
@@ -273,8 +304,8 @@
         return carry
 
     carry = lax.fori_loop(0, ni - 1, upper, carry, unroll=5)
-    x_copies = []
-    swap(x_copies, wx.at[2:4], wx.at[ni + 2 : ni + 4], fsend.at[8], frecv.at[8], (-1, 0, 0))
+    around = []
+    face_swap(around, (-1, 0, 0))
     arrive(far)
     for h in range(2):
         layer(h, ni, 0, lambda m, h: rx[m, :, 128 * h : 128 * h + 128], rz[1, 0])
@@ -290,7 +321,7 @@
         for h in range(2):
             carry = unit(ni - 1, q, h, *carry)
     c_sum, v_sum = carry
-    swap(x_copies, wx.at[ni : ni + 2], wx.at[0:2], fsend.at[9], frecv.at[9], (1, 0, 0))
+    face_swap(around, (1, 0, 0))
 
     def share(base, mine, value, group):
         sums[base + mine] = value
@@ -321,85 +352,108 @@
 
     partial = jnp.where(iota((1, 128), 1) < 64, fold(c_sum), fold(v_sum))
     x_sums = share(0, me["gx"], partial, line)
-    arrive(x_copies)
-
-    def smooth_x(i, carry):
-        lo, hi = carry
-        s = 3.0 * wx[i + 2] + 2.0 * (wx[i + 1] + wx[i + 3]) + (wx[i] + wx[i + 4])
-        wy[i, 8 : 8 + nj, :] = s
-        for at in range(2):
-            yslo[at, pl.ds(i, 1), :] = s[at : at + 1]
-            yshi[at, pl.ds(i, 1), :] = s[nj - 2 + at : nj - 1 + at]
-        mine = (lane >> 1) == i
-        lo = jnp.where(mine, pltpu.roll(s[:, 0:128], 2 * i, 1), lo)
-        hi = jnp.where(mine, pltpu.roll(s[:, nk - 128 : nk], lax.rem(2 * i + 2, 128), 1), hi)
-        return lo, hi
-
-    none = jnp.zeros((nj, 128), F32)
-    lo, hi = lax.fori_loop(0, ni, smooth_x, (none, none), unroll=4)
-    zslo[...] = lo
-    zshi[...] = hi
-    side_copies = []
-    for at, (b, c) in enumerate(SIDE_STEPS):
-        if c:
-            rows = (slice(nj - 8, nj), slice(0, nj), slice(0, 8))[1 - b]
-            to = (slice(0, 8), slice(8, 8 + nj), slice(8 + nj, 16 + nj))[1 - b]
-            src = (zslo if c < 0 else zshi).at[rows]
-            dst = rzz.at[1 if c < 0 else 0, to]
-        else:
-            src, dst = (yslo, ryhi) if b < 0 else (yshi, rylo)
-        swap(side_copies, src, dst, fsend.at[at], frecv.at[at], (0, b, c))
+
+    zlo = zhi = jnp.zeros((nj, 128), F32)
+    for i in range(ni):
+        mine = (lane >> 1) == i + 2
+        plane = wx[i + 2]
+        zlo = jnp.where(mine, pltpu.roll(plane[:, 0:128], 2 * i + 4, 1), zlo)
+        zhi = jnp.where(mine, pltpu.roll(plane[:, nk - 128 : nk], (2 * i + 6) % 128, 1), zhi)
+        for t in range(2):
+            for top, row in enumerate((t, nj - 2 + t)):
+                line_at = wx[i + 2, row : row + 1, :]
+                ysend[top, t, i : i + 1, :] = line_at
+                if i < 2 or i >= ni - 2:
+                    p = i if i < 2 else i - ni + 2
+                    corner_send[int(i >= 2), top, 2 * p + t : 2 * p + t + 1, :] = line_at
+    zsend[0] = zlo
+    zsend[1] = zhi
+    for step in AROUND:
+        if step[1] or step[2]:
+            face_swap(around, step)
+
+    def spread_x(i):
+        return 3.0 * wx[i + 2] + 2.0 * (wx[i + 1] + wx[i + 3]) + (wx[i] + wx[i + 4])
+
+    def spread_z(xs):
+        x = jnp.concatenate(xs, 0)
+        high = x.astype(BF16)
+        low = (x - high.astype(F32)).astype(BF16)
+        both = jnp.dot(jnp.concatenate([high, low], 0), band[...], preferred_element_type=F32)
+        return both[: x.shape[0]] + both[x.shape[0] :]
+
+    def planes_xz(group):
+        done = spread_z([spread_x(i) for i in group])
+        for at, i in enumerate(group):
+            for h in range(2):
+                wy[i, h, 8 : 8 + nj, :] = done[nj * at : nj * at + nj, 128 * h : 128 * h + 128]
+
+    for first in range(2, ni - 2, 4):
+        planes_xz(range(first, min(first + 4, ni - 2)))
     all_sums = share(n["gx"], me["gy"] * nz + me["gz"], gather(0, x_sums), sheet)
-    arrive(side_copies)
-
-    def smooth_rows(ref, at):
-        return (
-            3.0 * ref[at, 8 : 8 + nj, :]
-            + 2.0 * (ref[at, 7 : 7 + nj, :] + ref[at, 9 : 9 + nj, :])
-            + (ref[at, 6 : 6 + nj, :] + ref[at, 10 : 10 + nj, :])
+    arrive(around)
+
+    planes_xz((0, 1, ni - 2, ni - 1))
+    lines = []
+    for at in range(4):
+        side, t = at >> 1, at & 1
+        for p in range(2):
+            rows_in[at, 6 + p : 7 + p, :] = corner_in[0, side, 2 * p + t : 2 * p + t + 1, :]
+            rows_in[at, 8 + ni + p : 9 + ni + p, :] = corner_in[1, side, 2 * p + t : 2 * p + t + 1, :]
+        x = [rows_in[at, 6 + d : 6 + d + ni, :] for d in range(5)]
+        lines.append(3.0 * x[2] + 2.0 * (x[1] + x[3]) + (x[0] + x[4]))
+    done = spread_z(lines)
+    for at in range(4):
+        yrow[at] = done[ni * at : ni * at + ni]
+
+    wide = iota((nj + 16, 128), 1)
+    even = lax.rem(lane, 2) == 0
+    rims = []
+    for side in range(2):
+        x = jnp.where(
+            wide < 4,
+            pltpu.roll(rzz[side, 0], 128 - 2 * ni, 1),
+            jnp.where(wide < 2 * ni + 4, rzz[side, 1], pltpu.roll(rzz[side, 2], 2 * ni, 1)),
         )
-
-    for side in range(2):
-        packs[side] = smooth_rows(rzz, side)
-
-    def smooth_y(i, carry):
-        for at in range(2):
-            wy[i, 6 + at : 7 + at, :] = rylo[at, pl.ds(i, 1), :]
-            wy[i, 8 + nj + at : 9 + nj + at, :] = ryhi[at, pl.ds(i, 1), :]
-        out[i] = smooth_rows(wy, i)
-        return carry
-
-    lax.fori_loop(0, ni, smooth_y, 0, unroll=4)
+        x = (
+            3.0 * x
+            + 2.0 * (pltpu.roll(x, 2, 1) + pltpu.roll(x, 126, 1))
+            + (pltpu.roll(x, 4, 1) + pltpu.roll(x, 124, 1))
+        )
+        rzs[side] = x
+        y = [rzs[side, 6 + d : 6 + d + nj, :] for d in range(5)]
+        y = 3.0 * y[2] + 2.0 * (y[1] + y[3]) + (y[0] + y[4])
+        y = y + jnp.where(even, 0.0, 2.0 * pltpu.roll(y, 1, 1)) if side else (
+            y + jnp.where(even, 2.0 * pltpu.roll(y, 127, 1), 0.0)
+        )
+        rims.append(y)
+
+    for i in range(ni):
+        for h in range(2):
+            half = slice(128 * h, 128 * h + 128)
+            for t in range(2):
+                wy[i, h, 6 + t : 7 + t, :] = yrow[t, i : i + 1, half]
+                wy[i, h, 8 + nj + t : 9 + nj + t, :] = yrow[2 + t, i : i + 1, half]
+            y = [wy[i, h, 6 + d : 6 + d + nj, :] for d in range(5)]
+            y = 3.0 * y[2] + 2.0 * (y[1] + y[3]) + (y[0] + y[4])
+            if h:
+                rim = jnp.where(lane >= 126, pltpu.roll(rims[1], 122 - 2 * i, 1), 0.0)
+            else:
+                rim = jnp.where(lane < 2, pltpu.roll(rims[0], 124 - 2 * i, 1), 0.0)
+            out[i, :, half] = y + rim
     totals[...] = gather(n["gx"], all_sums)
-    for copies in (beside, below, far, x_copies, side_copies):
+    for copies in (beside, below, far, around):
         finish(copies)
 
 
-def last_pass(cells, field, packs, totals, out, comp, vol):
-    ni, nj, nk = field.shape
+def last_pass(cells, field, totals, out, comp, vol, sem):
+    copy = pltpu.make_async_copy(field, out, sem.at[0])
+    copy.start()
     both = totals[...]
     first = iota((1, 128), 1) < 64
     comp[0, 0] = jnp.sum(jnp.where(first, both, 0.0)) / cells
     vol[0, 0] = jnp.sum(jnp.where(first, 0.0, both)) / cells
-    lanes = iota((nj, nk), 1)
-    even = lax.rem(iota((nj, 128), 1), 2) == 0
-    left, right = packs[0], packs[1]
-    left = jnp.where(even, left + 2.0 * pltpu.roll(left, 127, 1), left)
-    right = jnp.where(even, right, right + 2.0 * pltpu.roll(right, 1, 1))
-    apart = jnp.abs(iota((nk, nk), 0) - iota((nk, nk), 1))
-    band = jnp.maximum(3 - apart, 0).astype(F32).astype(BF16)
-
-    def twice(x):
-        return jnp.concatenate([x, x], 1)
-
-    for i in range(ni):
-        t = field[i]
-        high = t.astype(BF16)
-        low = (t - high.astype(F32)).astype(BF16)
-        own = jnp.dot(high, band, preferred_element_type=F32) + jnp.dot(low, band, preferred_element_type=F32)
-        lo = twice(pltpu.roll(left, (128 - 2 * i) % 128, 1))
-        hi = twice(pltpu.roll(right, 126 - 2 * i, 1))
-        out[i] = own + jnp.where(lanes < 2, lo, jnp.where(lanes >= nk - 2, hi, 0.0))
+    copy.wait()
 
 
 def on_device(sizes, displacement, density, stiffness):
@@ -414,23 +468,22 @@
         (2, 3, ni + 1, 2, nj + 8, 128), (2, nj // 16, ni + 1, 8, nk), (6, ni, nk), (6, ni, nk), (nj, nk),
     ]
     later = [
-        (ni + 4, nj, nk), (ni, nj + 16, nk),
-        (2, ni, nk), (2, ni, nk), (2, ni, nk), (2, ni, nk),
-        (nj, 128), (nj, 128), (2, nj + 16, 128), (members, 1, 128),
+        (ni + 4, nj, nk), (ni, 2, nj + 16, 128),
+        (2, 2, ni, nk), (2, 2, 8, nk), (2, nj, 128), (4, ni + 16, nk), (2, 2, 8, nk),
+        (2, 3, nj + 16, 128), (2, nj + 16, 128), (4, ni, nk), (members, 1, 128),
     ]
-    field, packs, totals = pl.pallas_call(
+    field, totals = pl.pallas_call(
         functools.partial(kernel, sizes),
         out_shape=(
             jax.ShapeDtypeStruct((ni, nj, nk), F32),
-            jax.ShapeDtypeStruct((2, nj, 128), F32),
             jax.ShapeDtypeStruct((1, 128), F32),
         ),
         in_specs=[hbm] * 3,
-        out_specs=(vmem, vmem, vmem),
+        out_specs=(vmem, vmem),
         scratch_shapes=[pltpu.VMEM(shape, F32) for shape in scratch]
-        + [pltpu.VMEM((2, nj // 16, ni + 1, 48, nk), BF16), pltpu.VMEM((192, 256), BF16)]
+        + [pltpu.VMEM((2, nj // 16, ni + 1, 48, nk), BF16), pltpu.VMEM((192, 256), BF16), pltpu.VMEM((nk, nk), BF16)]
         + [pltpu.VMEM(shape, F32) for shape in later]
-        + [pltpu.SemaphoreType.DMA((count,)) for count in (3, 7, 7, 10, 10, members, members)],
+        + [pltpu.SemaphoreType.DMA((count,)) for count in (3, 7, 7, 26, 26, members, members)],
         compiler_params=pltpu.CompilerParams(
             collective_id=0, has_side_effects=True, vmem_limit_bytes=24 * 1024 * 1024
         ),
@@ -443,10 +496,11 @@
             jax.ShapeDtypeStruct((1, 1), F32),
             jax.ShapeDtypeStruct((1, 1), F32),
         ),
-        in_specs=[vmem] * 3,
-        out_specs=(vmem, smem, smem),
+        in_specs=[vmem] * 2,
+        out_specs=(hbm, smem, smem),
+        scratch_shapes=[pltpu.SemaphoreType.DMA((1,))],
         compiler_params=pltpu.CompilerParams(vmem_limit_bytes=24 * 1024 * 1024),
-    )(field, packs, totals)
+    )(field, totals)
     return filtered, comp.reshape(()), vol.reshape(())
 
 

time: 20.8 us -> 20.4 us (0.981)
  Pallas kernels: 20 us -> 19.7 us
    pallas_call x1, Pallas kernels: 1.66 us -> 1.33 us  [on_device(): pl.pallas_call(functools.partial(last_pass, cells), out_shape=(jax.ShapeD...]
where the time goes in v3:
time: 20.4 us; the launch traced here: 20.3 us
  Pallas kernels  19.7 us (97%)
  between operations  0.64 us (3%)
    pallas_call x1, Pallas kernels, on_device(): pl.pallas_call(functools.partial(kernel, sizes), out_shape=(jax.ShapeDtyp...  18.3 us
    pallas_call x1, Pallas kernels, on_device(): pl.pallas_call(functools.partial(last_pass, cells), out_shape=(jax.ShapeD...  1.33 us

profile of v3, /device:TPU:0, one launch (start us, length us, event | category | flops | bytes accessed | tf_op | source)
XLA Modules:
  0.0 20.3 jit_solution(12985459512410860640)
XLA Ops:
  0.6 18.3 %shard_map.58 = (f32[16,32,256]{2,1,0:T(8,128)S(1)}, f32[1,128]{1,0:T(1,128)S(1)}) custom-call(f32[3,16,32,256]{3,2,1,0:T(8,128)} %u_hbm.1, f32[16,32,256]{2,1,0:T(8,128)} %rho_hbm.1, f32[24,24]{1,0:T(8,128)} %stiff_hbm.1), custom_call_target="tpu_custom_call" | custom-call | tf_op jit(solution)/shard_map/pallas_call | solution.py:475
  19.0 1.3 %shard_map.59 = (f32[16,32,256]{2,1,0:T(8,128)}, f32[1,1]{1,0:T(1,128)}, f32[1,1]{1,0:T(1,128)}) custom-call(f32[16,32,256]{2,1,0:T(8,128)S(1)} %get-tuple-element.8.field, f32[1,128]{1,0:T(1,128)S(1)} %get-tuple-element.9.totals), custom_call_target="tpu_custom_call" | custom-call | tf_op jit(solution)/shard_map/pallas_call | solution.py:492

commit v4 on v3

--- a/solution.py
+++ b/solution.py
@@ -14,6 +14,7 @@
 F32 = jnp.float32
 BF16 = jnp.bfloat16
 NODE_STEPS = [(a, b, c) for a in (0, 1) for b in (0, 1) for c in (0, 1) if a + b + c]
+FEW = 64
 AROUND = [(a, b, c) for a in (-1, 0, 1) for b in (-1, 0, 1) for c in (-1, 0, 1) if a or b or c]
 
 
@@ -61,7 +62,7 @@
     u, rho, stiff, rx, ry, rxy, rz, ys, yd, zs,
     field, edge, line_f, line_u, inv, parts, weights, band, wx, wy,
     ysend, corner_send, zsend, rows_in, corner_in, rzz, rzs, yrow,
-    sums, insem, nsend, nrecv, fsend, frecv, gsend, grecv,
+    sums, insem, nsend, nrecv, fsend, frecv, gsend, grecv, known,
 ):
     ni, nj, nk = rho.shape
     n = dict(zip(AXES, sizes))
@@ -71,7 +72,8 @@
     up = {axis: me[axis] < n[axis] - 1 for axis in AXES}
 
     loads = []
-    for at, (src, dst) in enumerate(((stiff_hbm, stiff), (u_hbm, u), (rho_hbm, rho))):
+    halves = [(u_hbm.at[:, :, :, at : at + 128], u.at[:, :, :, at : at + 128]) for at in (0, 128)]
+    for at, (src, dst) in enumerate([(stiff_hbm, stiff)] + halves + [(rho_hbm, rho)]):
         copy = pltpu.make_async_copy(src, dst, insem.at[at])
         copy.start()
         loads.append(copy)
@@ -88,23 +90,49 @@
     def minus(step):
         return tuple(-s for s in step)
 
+    everyone = n["gx"] * ny * nz
+    mine = (me["gx"] * ny + me["gy"]) * nz + me["gz"]
+
+    def place(at):
+        return {"gx": at // (ny * nz), "gy": lax.rem(at // nz, ny), "gz": lax.rem(at, nz)}
+
     line = [{"gx": lax.rem(me["gx"] + off, n["gx"])} for off in range(1, n["gx"])]
     sheet = [
         {"gy": lax.rem(me["gy"] + off // nz, ny), "gz": lax.rem(me["gz"] + off % nz, nz)}
         for off in range(1, ny * nz)
     ]
+    if everyone <= FEW:
+        group = [place(lax.rem(mine + off, everyone)) for off in range(1, everyone)]
+        stages = [(mine, group)]
+        met = [(ids, True, mine + off < everyone) for off, ids in enumerate(group, 1)]
+    else:
+        stages = [(me["gx"], line), (me["gy"] * nz + me["gz"], sheet)]
+        met = [(ids, True, me["gx"] + off < n["gx"]) for off, ids in enumerate(line, 1)]
+        met += [(ids, True, me["gy"] * nz + me["gz"] + off < ny * nz) for off, ids in enumerate(sheet, 1)]
+        met += [hop(step) + (step[0] > 0,) for step in AROUND if step[0] and (step[1] or step[2])]
+
+    def greet(semaphore, upward):
+        for ids, ok, later in met:
+            flag = later if upward else jnp.logical_not(later)
+
+            @pl.when(jnp.logical_and(ok, flag))
+            def _():
+                pl.semaphore_signal(semaphore, inc=1, device_id=ids, device_id_type=MESH)
+
+    def count(upward):
+        total = 0
+        for _, ok, later in met:
+            flag = later if upward else jnp.logical_not(later)
+            total = total + jnp.where(jnp.logical_and(ok, flag), 1, 0)
+        return total
+
+    def hear(semaphore, amount):
+        @pl.when(amount > 0)
+        def _():
+            pl.semaphore_wait(semaphore, amount)
+
     barrier = pltpu.get_barrier_semaphore()
-    for ids in line + sheet:
-        pl.semaphore_signal(barrier, inc=1, device_id=ids, device_id_type=MESH)
-    peers = len(line) + len(sheet)
-    for step in AROUND:
-        if step[0] and (step[1] or step[2]):
-            ids, ok = hop(step)
-            peers = peers + jnp.where(ok, 1, 0)
-
-            @pl.when(ok)
-            def _():
-                pl.semaphore_signal(barrier, inc=1, device_id=ids, device_id_type=MESH)
+    greet(barrier, True)
 
     def node_route(step):
         a, b, c = step
@@ -112,7 +140,7 @@
             return (zs.at[0:8], rz.at[a, b, 0:8]) if b else (zs, rz.at[a, b])
         if b:
             return (yd, rxy) if a else (ys, ry)
-        return u_hbm.at[:, 0], rx
+        return u.at[:, 0], rx
 
     def face_route(step):
         a, b, c = step
@@ -141,8 +169,6 @@
     band[...] = jnp.maximum(3 - apart, 0).astype(F32).astype(BF16)
     edge[...] = jnp.zeros(edge.shape, F32)
 
-    pl.semaphore_wait(barrier, peers)
-
     def swap(copies, src, dst, send_sem, recv_sem, step):
         ids, sends = hop(step)
         copy = pltpu.make_async_remote_copy(
@@ -183,7 +209,6 @@
         src, dst = face_route(step)
         swap(copies, src, dst, fsend.at[at], frecv.at[at], step)
 
-    node_swap((1, 0, 0))
     loads[0].wait()
     weights[...] = band_weights(stiff[...])
     loads[1].wait()
@@ -193,16 +218,16 @@
         column = u[at // ni, at % ni, :, 0:128]
         packed = jnp.where(lane == at, pltpu.roll(column, at, 1) if at else column, packed)
     zs[...] = packed
-    for step in NODE_STEPS:
-        if step[2]:
-            node_swap(step)
+    loads[2].wait()
     yd[...] = jnp.zeros(yd.shape, F32)
     for m in range(3):
         for i in range(ni):
             ys[m, i : i + 1, :] = u[m, i, 0:1, :]
         yd[m : m + 1, :] = u[m, 0, 0:1, :]
-    node_swap((0, 1, 0))
-    node_swap((1, 1, 0))
+    hear(barrier, mine if everyone <= FEW else count(False))
+    for step in sorted(NODE_STEPS, key=lambda step: (sum(step), step)):
+        node_swap(step)
+    greet(known.at[0], False)
 
     last = iota((nj, 128), 1) == 127
     nq = nj // 16
@@ -231,17 +256,16 @@
     def own(i):
         return lambda m, h: u[m, i, :, 128 * h : 128 * h + 128]
 
-    def next_row(c, m, to, x, f):
+    def next_row(c, m, to, h, x):
+        field[c, m, to, h, nj : nj + 1, :] = sharp(x)
+        edge[h, nq - 1, to, 3 * c + m : 3 * c + m + 1, 128:256] = x
+
+    def own_row(i, carry):
+        at = pl.ds(i, 1)
         for h in range(2):
-            half = slice(128 * h, 128 * h + 128)
-            field[c, m, to, h, nj : nj + 1, :] = f[:, half]
-            edge[h, nq - 1, to, 3 * c + m : 3 * c + m + 1, 128:256] = x[:, half]
-
-    def own_row(i, carry):
-        for c in range(2):
-            for m in range(3):
-                at = pl.ds(i, 1)
-                next_row(c, m, i, line_u[3 * c + m, at, :], line_f[3 * c + m, at, :])
+            for cm in range(6):
+                field[cm // 3, cm % 3, i, h, nj : nj + 1, :] = line_f[h, cm, at, :]
+                edge[h, nq - 1, i, cm : cm + 1, 128:256] = line_u[h, cm, at, :]
         return carry
 
     none8 = jnp.zeros((8, nk), F32)
@@ -275,7 +299,7 @@
 
         return body
 
-    loads[2].wait()
+    loads[3].wait()
     inv[...] = 1.0 / (
         line_sum(me["gy"] * nj + iota((nj, nk), 0), ny * nj)
         * line_sum(me["gz"] * nk + iota((nj, nk), 1), nz * nk)
@@ -287,15 +311,20 @@
     layer(1, 0, 0, own(0), rz[0, 0])
     carry = lax.fori_loop(0, ni - 1, sweep(1), carry, unroll=5)
     arrive(below)
-    for m in range(3):
-        base = ry[m]
-        mine = iota((ni, 128), 1) == iota((ni, 128), 0) + m * ni
-        corner = jnp.sum(jnp.where(mine, rz[0, 1, 0:1, :], 0.0), axis=1, keepdims=True)
-        moved = jnp.where(iota((ni, nk), 1) == nk - 1, corner, pltpu.roll(base, nk - 1, 1))
-        for c, x in enumerate((base, moved)):
-            line_u[3 * c + m] = x
-            line_f[3 * c + m] = sharp(x)
-    lax.fori_loop(0, ni, own_row, 0, unroll=4)
+
+    def row_pair(h):
+        for m in range(3):
+            base = ry[m]
+            if h:
+                mine = iota((ni, 128), 1) == iota((ni, 128), 0) + m * ni
+                side = jnp.sum(jnp.where(mine, rz[0, 1, 0:1, :], 0.0), axis=1, keepdims=True)
+            else:
+                side = pltpu.roll(base[:, 128:256], 127, 1)
+            x = base[:, 128 * h : 128 * h + 128]
+            moved = jnp.where(iota((ni, 128), 1) == 127, side, pltpu.roll(x, 127, 1))
+            for c, y in enumerate((x, moved)):
+                line_u[h, 3 * c + m] = y
+                line_f[h, 3 * c + m] = sharp(y)
 
     def upper(i, carry):
         for q in range(1, nq):
@@ -303,7 +332,31 @@
                 carry = unit(i, q, h, *carry)
         return carry
 
+    for h in range(2):
+        row_pair(h)
+    lax.fori_loop(0, ni, own_row, 0, unroll=4)
     carry = lax.fori_loop(0, ni - 1, upper, carry, unroll=5)
+    zlo = zhi = jnp.zeros((nj, 128), F32)
+
+    def pack(i, zlo, zhi):
+        slot = (lane >> 1) == i + 2
+        plane = wx[i + 2]
+        zlo = jnp.where(slot, pltpu.roll(plane[:, 0:128], 2 * i + 4, 1), zlo)
+        zhi = jnp.where(slot, pltpu.roll(plane[:, nk - 128 : nk], (2 * i + 6) % 128, 1), zhi)
+        for t in range(2):
+            for top, row in enumerate((t, nj - 2 + t)):
+                line_at = wx[i + 2, row : row + 1, :]
+                ysend[top, t, i : i + 1, :] = line_at
+                if i < 2 or i >= ni - 2:
+                    p = i if i < 2 else i - ni + 2
+                    corner_send[int(i >= 2), top, 2 * p + t : 2 * p + t + 1, :] = line_at
+        return zlo, zhi
+
+    for i in range(ni - 1):
+        zlo, zhi = pack(i, zlo, zhi)
+    zsend[0] = zlo
+    zsend[1] = zhi
+    hear(known.at[0], everyone - 1 - mine if everyone <= FEW else count(True))
     around = []
     face_swap(around, (-1, 0, 0))
     arrive(far)
@@ -316,34 +369,34 @@
             iota((1, nk), 1) == nk - 1, jnp.concatenate([side, side], 1), pltpu.roll(row, nk - 1, 1)
         )
         for c, x in enumerate((row, moved)):
-            next_row(c, m, ni, x, sharp(x))
+            for h in range(2):
+                next_row(c, m, ni, h, x[:, 128 * h : 128 * h + 128])
     for q in range(nq):
         for h in range(2):
             carry = unit(ni - 1, q, h, *carry)
     c_sum, v_sum = carry
-    face_swap(around, (1, 0, 0))
-
-    def share(base, mine, value, group):
-        sums[base + mine] = value
-        copies = []
-        for off, ids in enumerate(group):
-            copy = pltpu.make_async_remote_copy(
-                src_ref=sums.at[base + mine], dst_ref=sums.at[base + mine],
-                send_sem=gsend.at[base + off], recv_sem=grecv.at[base + off],
+
+    def share(at, value):
+        slot, group = stages[at]
+        base = sum(len(stage[1]) + 1 for stage in stages[:at])
+        sums[base + slot] = value
+        for ids in group:
+            pltpu.make_async_remote_copy(
+                src_ref=sums.at[base + slot], dst_ref=sums.at[base + slot],
+                send_sem=gsend.at[at], recv_sem=grecv.at[at],
                 device_id=ids, device_id_type=MESH,
-            )
-            copy.start()
-            copies.append(copy)
-        return copies
-
-    def gather(base, copies):
-        for copy in copies:
-            copy.wait()
+            ).start()
+
+    def gather(at):
+        size = len(stages[at][1])
+        base = sum(len(stage[1]) + 1 for stage in stages[:at])
+        every = sums.at[base : base + size]
+        pltpu.make_async_copy(every, every, grecv.at[at]).wait()
+        pltpu.make_async_copy(every, every, gsend.at[at]).wait()
         total = sums[base]
-        for at in range(1, len(copies) + 1):
-            total = total + sums[base + at]
+        for slot in range(1, size + 1):
+            total = total + sums[base + slot]
         return total
-
 
     def fold(x):
         row = jnp.sum(x, axis=0, keepdims=True)
@@ -351,21 +404,10 @@
         return row + pltpu.roll(row, 64, 1)
 
     partial = jnp.where(iota((1, 128), 1) < 64, fold(c_sum), fold(v_sum))
-    x_sums = share(0, me["gx"], partial, line)
-
-    zlo = zhi = jnp.zeros((nj, 128), F32)
-    for i in range(ni):
-        mine = (lane >> 1) == i + 2
-        plane = wx[i + 2]
-        zlo = jnp.where(mine, pltpu.roll(plane[:, 0:128], 2 * i + 4, 1), zlo)
-        zhi = jnp.where(mine, pltpu.roll(plane[:, nk - 128 : nk], (2 * i + 6) % 128, 1), zhi)
-        for t in range(2):
-            for top, row in enumerate((t, nj - 2 + t)):
-                line_at = wx[i + 2, row : row + 1, :]
-                ysend[top, t, i : i + 1, :] = line_at
-                if i < 2 or i >= ni - 2:
-                    p = i if i < 2 else i - ni + 2
-                    corner_send[int(i >= 2), top, 2 * p + t : 2 * p + t + 1, :] = line_at
+    share(0, partial)
+    face_swap(around, (1, 0, 0))
+
+    zlo, zhi = pack(ni - 1, zsend[0], zsend[1])
     zsend[0] = zlo
     zsend[1] = zhi
     for step in AROUND:
@@ -390,7 +432,8 @@
 
     for first in range(2, ni - 2, 4):
         planes_xz(range(first, min(first + 4, ni - 2)))
-    all_sums = share(n["gx"], me["gy"] * nz + me["gz"], gather(0, x_sums), sheet)
+    for at in range(1, len(stages)):
+        share(at, gather(at - 1))
     arrive(around)
 
     planes_xz((0, 1, ni - 2, ni - 1))
@@ -441,31 +484,36 @@
             else:
                 rim = jnp.where(lane < 2, pltpu.roll(rims[0], 124 - 2 * i, 1), 0.0)
             out[i, :, half] = y + rim
-    totals[...] = gather(n["gx"], all_sums)
     for copies in (beside, below, far, around):
         finish(copies)
-
-
-def last_pass(cells, field, totals, out, comp, vol, sem):
+    totals[...] = gather(len(stages) - 1)
+
+
+def last_pass(cells, field, totals, out, comp, vol, ends, sem):
     copy = pltpu.make_async_copy(field, out, sem.at[0])
     copy.start()
     both = totals[...]
     first = iota((1, 128), 1) < 64
-    comp[0, 0] = jnp.sum(jnp.where(first, both, 0.0)) / cells
-    vol[0, 0] = jnp.sum(jnp.where(first, 0.0, both)) / cells
+    ends[0] = jnp.sum(jnp.where(first, both, 0.0), axis=1, keepdims=True) / cells
+    ends[1] = jnp.sum(jnp.where(first, 0.0, both), axis=1, keepdims=True) / cells
+    small = [pltpu.make_async_copy(ends.at[at], dst, sem.at[1 + at]) for at, dst in enumerate((comp, vol))]
+    for one in small:
+        one.start()
+    for one in small:
+        one.wait()
     copy.wait()
 
 
 def on_device(sizes, displacement, density, stiffness):
     ni, nj, nk = density.shape
     vmem = pl.BlockSpec(memory_space=pltpu.VMEM)
-    smem = pl.BlockSpec(memory_space=pltpu.SMEM)
     hbm = pl.BlockSpec(memory_space=pltpu.HBM)
-    members = sizes[0] + sizes[1] * sizes[2]
+    everyone = sizes[0] * sizes[1] * sizes[2]
+    members = everyone if everyone <= FEW else sizes[0] + sizes[1] * sizes[2]
     scratch = [
         displacement.shape, density.shape, stiffness.shape,
         (3, nj, nk), (3, ni, nk), (8, nk), (2, 2, nj, 128), (3, ni, nk), (8, nk), (nj, 128),
-        (2, 3, ni + 1, 2, nj + 8, 128), (2, nj // 16, ni + 1, 8, nk), (6, ni, nk), (6, ni, nk), (nj, nk),
+        (2, 3, ni + 1, 2, nj + 8, 128), (2, nj // 16, ni + 1, 8, nk), (2, 6, ni, 128), (2, 6, ni, 128), (nj, nk),
     ]
     later = [
         (ni + 4, nj, nk), (ni, 2, nj + 16, 128),
@@ -483,7 +531,8 @@
         scratch_shapes=[pltpu.VMEM(shape, F32) for shape in scratch]
         + [pltpu.VMEM((2, nj // 16, ni + 1, 48, nk), BF16), pltpu.VMEM((192, 256), BF16), pltpu.VMEM((nk, nk), BF16)]
         + [pltpu.VMEM(shape, F32) for shape in later]
-        + [pltpu.SemaphoreType.DMA((count,)) for count in (3, 7, 7, 26, 26, members, members)],
+        + [pltpu.SemaphoreType.DMA((count,)) for count in (4, 7, 7, 26, 26, 2, 2)]
+        + [pltpu.SemaphoreType.REGULAR((1,))],
         compiler_params=pltpu.CompilerParams(
             collective_id=0, has_side_effects=True, vmem_limit_bytes=24 * 1024 * 1024
         ),
@@ -497,8 +546,8 @@
             jax.ShapeDtypeStruct((1, 1), F32),
         ),
         in_specs=[vmem] * 2,
-        out_specs=(hbm, smem, smem),
-        scratch_shapes=[pltpu.SemaphoreType.DMA((1,))],
+        out_specs=(hbm, hbm, hbm),
+        scratch_shapes=[pltpu.VMEM((2, 1, 1), F32), pltpu.SemaphoreType.DMA((3,))],
         compiler_params=pltpu.CompilerParams(vmem_limit_bytes=24 * 1024 * 1024),
     )(field, totals)
     return filtered, comp.reshape(()), vol.reshape(())

time: 20.4 us -> 18.2 us (0.89)
  Pallas kernels: 19.7 us -> 17.5 us
    pallas_call x1, Pallas kernels: 18.3 us -> 16.6 us  [on_device(): pl.pallas_call(functools.partial(kernel, sizes), out_shape=(jax.ShapeDtyp...]
    pallas_call x1, Pallas kernels: 1.33 us -> 0.82 us  [on_device(): pl.pallas_call(functools.partial(last_pass, cells), out_shape=(jax.ShapeD...]
where the time goes in v4:
time: 18.2 us; the launch traced here: 18.1 us
  Pallas kernels  17.5 us (96%)
  between operations  0.64 us (4%)
    pallas_call x1, Pallas kernels, on_device(): pl.pallas_call(functools.partial(kernel, sizes), out_shape=(jax.ShapeDtyp...  16.6 us
    pallas_call x1, Pallas kernels, on_device(): pl.pallas_call(functools.partial(last_pass, cells), out_shape=(jax.ShapeD...  0.82 us

profile of v4, /device:TPU:0, one launch (start us, length us, event | category | flops | bytes accessed | tf_op | source)
XLA Modules:
  0.0 18.1 jit_solution(5377753061605995679)
XLA Ops:
  0.6 16.6 %shard_map.58 = (f32[16,32,256]{2,1,0:T(8,128)S(1)}, f32[1,128]{1,0:T(1,128)S(1)}) custom-call(f32[3,16,32,256]{3,2,1,0:T(8,128)} %u_hbm.1, f32[16,32,256]{2,1,0:T(8,128)} %rho_hbm.1, f32[24,24]{1,0:T(8,128)} %stiff_hbm.1), custom_call_target="tpu_custom_call" | custom-call | tf_op jit(solution)/shard_map/pallas_call | solution.py:523
  17.3 0.8 %shard_map.59 = (f32[16,32,256]{2,1,0:T(8,128)}, f32[1,1]{1,0:T(1,128)}, f32[1,1]{1,0:T(1,128)}) custom-call(f32[16,32,256]{2,1,0:T(8,128)S(1)} %get-tuple-element.8.field, f32[1,128]{1,0:T(1,128)S(1)} %get-tuple-element.9.totals), custom_call_target="tpu_custom_call" | custom-call | tf_op jit(solution)/shard_map/pallas_call | solution.py:541

commit v5 on v4

--- a/solution.py
+++ b/solution.py
@@ -60,7 +60,7 @@
 def kernel(
     sizes, u_hbm, rho_hbm, stiff_hbm, out, totals,
     u, rho, stiff, rx, ry, rxy, rz, ys, yd, zs,
-    field, edge, line_f, line_u, inv, parts, weights, band, wx, wy,
+    field, edge, line_f, line_u, inv, inv_x, parts, weights, band, wx, wy,
     ysend, corner_send, zsend, rows_in, corner_in, rzz, rzs, yrow,
     sums, insem, nsend, nrecv, fsend, frecv, gsend, grecv, known,
 ):
@@ -94,6 +94,7 @@
     mine = (me["gx"] * ny + me["gy"]) * nz + me["gz"]
 
     def place(at):
+        at = jnp.int32(at)
         return {"gx": at // (ny * nz), "gy": lax.rem(at // nz, ny), "gz": lax.rem(at, nz)}
 
     line = [{"gx": lax.rem(me["gx"] + off, n["gx"])} for off in range(1, n["gx"])]
@@ -102,29 +103,11 @@
         for off in range(1, ny * nz)
     ]
     if everyone <= FEW:
-        group = [place(lax.rem(mine + off, everyone)) for off in range(1, everyone)]
-        stages = [(mine, group)]
-        met = [(ids, True, mine + off < everyone) for off, ids in enumerate(group, 1)]
+        others = [at + jnp.where(at >= mine, 1, 0) for at in range(everyone - 1)]
+        stages = [(mine, [place(at) for at in others])]
     else:
         stages = [(me["gx"], line), (me["gy"] * nz + me["gz"], sheet)]
-        met = [(ids, True, me["gx"] + off < n["gx"]) for off, ids in enumerate(line, 1)]
-        met += [(ids, True, me["gy"] * nz + me["gz"] + off < ny * nz) for off, ids in enumerate(sheet, 1)]
-        met += [hop(step) + (step[0] > 0,) for step in AROUND if step[0] and (step[1] or step[2])]
-
-    def greet(semaphore, upward):
-        for ids, ok, later in met:
-            flag = later if upward else jnp.logical_not(later)
-
-            @pl.when(jnp.logical_and(ok, flag))
-            def _():
-                pl.semaphore_signal(semaphore, inc=1, device_id=ids, device_id_type=MESH)
-
-    def count(upward):
-        total = 0
-        for _, ok, later in met:
-            flag = later if upward else jnp.logical_not(later)
-            total = total + jnp.where(jnp.logical_and(ok, flag), 1, 0)
-        return total
+    lead = mine == everyone - 1
 
     def hear(semaphore, amount):
         @pl.when(amount > 0)
@@ -132,7 +115,21 @@
             pl.semaphore_wait(semaphore, amount)
 
     barrier = pltpu.get_barrier_semaphore()
-    greet(barrier, True)
+    beyond = [n[axis] - 1 - me[axis] > 1 for axis in AXES]
+    beyond = jnp.logical_or(jnp.logical_or(beyond[0], beyond[1]), beyond[2])
+    lower = 0
+    for step in NODE_STEPS:
+        ids, ok = hop(step)
+        lower = lower + jnp.where(hop(minus(step))[1], 1, 0)
+
+        @pl.when(ok)
+        def _():
+            pl.semaphore_signal(barrier, inc=1, device_id=ids, device_id_type=MESH)
+
+    @pl.when(beyond)
+    def _():
+        pl.semaphore_signal(barrier, inc=1, device_id=place(everyone - 1), device_id_type=MESH)
+
 
     def node_route(step):
         a, b, c = step
@@ -156,18 +153,12 @@
             return ysend.at[int(hi_b)], rows_in.at[at : at + 2, 8 : 8 + ni]
         return (wx.at[ni : ni + 2], wx.at[0:2]) if hi_a else (wx.at[2:4], wx.at[ni + 2 : ni + 4])
 
-    def clear(dst, step):
-        @pl.when(jnp.logical_not(hop(step)[1]))
+    def clear(missing, *refs):
+        @pl.when(jnp.logical_not(missing))
         def _():
-            dst[...] = jnp.zeros(dst.shape, F32)
-
-    for step in NODE_STEPS:
-        clear(node_route(step)[1], step)
-    for step in AROUND:
-        clear(face_route(step)[1], minus(step))
-    apart = jnp.abs(iota((nk, nk), 0) - iota((nk, nk), 1))
-    band[...] = jnp.maximum(3 - apart, 0).astype(F32).astype(BF16)
-    edge[...] = jnp.zeros(edge.shape, F32)
+            for ref in refs:
+                ref[...] = jnp.zeros(ref.shape, F32)
+
 
     def swap(copies, src, dst, send_sem, recv_sem, step):
         ids, sends = hop(step)
@@ -224,19 +215,33 @@
         for i in range(ni):
             ys[m, i : i + 1, :] = u[m, i, 0:1, :]
         yd[m : m + 1, :] = u[m, 0, 0:1, :]
-    hear(barrier, mine if everyone <= FEW else count(False))
+    hear(barrier, jnp.where(lead, everyone - 1, lower))
     for step in sorted(NODE_STEPS, key=lambda step: (sum(step), step)):
         node_swap(step)
-    greet(known.at[0], False)
+
+    @pl.when(lead)
+    def _():
+        def greet(at, carry):
+            pl.semaphore_signal(known.at[0], inc=1, device_id=place(at), device_id_type=MESH)
+            return carry
+
+        lax.fori_loop(0, everyone - 1, greet, 0)
+
+    clear(up["gx"], rx, rxy, rz.at[1], wx.at[ni + 2 : ni + 4], corner_in.at[1], rzz.at[:, 2])
+    clear(up["gy"], ry, rxy, rz.at[:, 1, 0:8], rows_in.at[2:4], corner_in.at[:, 1], rzz.at[:, :, 8 + nj : 16 + nj])
+    clear(up["gz"], rz, rzz.at[1])
+    clear(down["gx"], wx.at[0:2], corner_in.at[0], rzz.at[:, 0])
+    clear(down["gy"], rows_in.at[0:2], corner_in.at[:, 0], rzz.at[:, :, 0:8])
+    clear(down["gz"], rzz.at[0])
+    apart = jnp.abs(iota((nk, nk), 0) - iota((nk, nk), 1))
+    band[...] = jnp.maximum(3 - apart, 0).astype(F32).astype(BF16)
+    edge[...] = jnp.zeros(edge.shape, F32)
 
     last = iota((nj, 128), 1) == 127
-    nq = nj // 16
+    nt = nj // 8
 
     def sharp(x):
         return x + (x - x.astype(BF16).astype(F32))
-
-    def pair(x, q):
-        return jnp.concatenate([x[16 * q : 16 * q + 8], x[16 * q + 8 : 16 * q + 16]], 1)
 
     def layer(h, to, at, source, col):
         for m in range(3):
@@ -246,59 +251,77 @@
             moved = jnp.where(last, pltpu.roll(side, turn, 1), pltpu.roll(x, 127, 1))
             for c, y in enumerate((x, moved)):
                 field[c, m, to, h, 0:nj, :] = sharp(y)
-                for jt in range(nj // 8 - 1):
-                    edge[h, jt // 2, to, 3 * c + m : 3 * c + m + 1, 128 * (jt % 2) : 128 * (jt % 2) + 128] = (
-                        y[8 * jt + 8 : 8 * jt + 9, :]
-                    )
-            for q in range(nq):
-                parts[h, q, to, 16 * m : 16 * m + 16, :] = jnp.concatenate([pair(x, q), pair(moved, q)], 0).astype(BF16)
+                for jt in range(nt - 1):
+                    edge[h, jt, to, 3 * c + m : 3 * c + m + 1, :] = y[8 * jt + 8 : 8 * jt + 9, :]
+            for jt in range(nt):
+                rows = slice(8 * jt, 8 * jt + 8)
+                parts[h, jt, to, 16 * m : 16 * m + 16, :] = jnp.concatenate([x[rows], moved[rows]], 0).astype(BF16)
 
     def own(i):
         return lambda m, h: u[m, i, :, 128 * h : 128 * h + 128]
 
     def next_row(c, m, to, h, x):
         field[c, m, to, h, nj : nj + 1, :] = sharp(x)
-        edge[h, nq - 1, to, 3 * c + m : 3 * c + m + 1, 128:256] = x
+        edge[h, nt - 1, to, 3 * c + m : 3 * c + m + 1, :] = x
 
     def own_row(i, carry):
         at = pl.ds(i, 1)
         for h in range(2):
             for cm in range(6):
                 field[cm // 3, cm % 3, i, h, nj : nj + 1, :] = line_f[h, cm, at, :]
-                edge[h, nq - 1, i, cm : cm + 1, 128:256] = line_u[h, cm, at, :]
+                edge[h, nt - 1, i, cm : cm + 1, :] = line_u[h, cm, at, :]
         return carry
 
     none8 = jnp.zeros((8, nk), F32)
 
-    def tile(h, q, p):
-        return [parts[h, q, p], jnp.concatenate([edge[h, q, p], none8], 0).astype(BF16)]
-
-    def unit(i, q, h, c_sum, v_sum):
-        half = slice(128 * h, 128 * h + 128)
-        rows = [slice(16 * q + 8 * t, 16 * q + 8 * t + 8) for t in range(2)]
-        data = tile(h, q, i) + tile(h, q, i + 1)
+    def both(take, tiles):
+        return jnp.concatenate([take(*tile) for tile in tiles], 1)
+
+    def unit(tiles, carry):
+        c_sum, v_sum = carry
+        data = []
+        for a in range(2):
+            data.append(both(lambda i, jt, h: parts[h, jt, i + a], tiles))
+            rim = both(lambda i, jt, h: edge[h, jt, i + a], tiles)
+            data.append(jnp.concatenate([rim, none8], 0).astype(BF16))
         product = jnp.dot(weights[...], jnp.concatenate(data + data, 0), preferred_element_type=F32)
         energy = None
         for r in range(24):
             m, a, b, c = r >> 3, (r >> 2) & 1, (r >> 1) & 1, r & 1
-            f = [field[c, m, i + a, h, 16 * q + 8 * t + b : 16 * q + 8 * t + b + 8, :] for t in range(2)]
-            term = product[8 * r : 8 * r + 8] * jnp.concatenate(f, 1)
+            f = both(lambda i, jt, h: field[c, m, i + a, h, 8 * jt + b : 8 * jt + b + 8, :], tiles)
+            term = product[8 * r : 8 * r + 8] * f
             energy = term if energy is None else energy + term
-        d = jnp.concatenate([rho[i, rows[t], half] for t in range(2)], 1)
-        scale = jnp.concatenate([inv[rows[t], half] for t in range(2)], 1)
-        inv_x = 1.0 / line_sum(jnp.full((8, nk), me["gx"] * ni + i, jnp.int32), n["gx"] * ni)
-        w = (-3.0 * (1.0 - VOID)) * d * d * energy * (inv_x * scale)
-        for t in range(2):
-            wx[i + 2, rows[t], half] = w[:, 128 * t : 128 * t + 128]
+
+        d = both(lambda i, jt, h: rho[i, 8 * jt : 8 * jt + 8, 128 * h : 128 * h + 128], tiles)
+        scale = both(
+            lambda i, jt, h: inv[8 * jt : 8 * jt + 8, 128 * h : 128 * h + 128] * inv_x[pl.ds(i, 1), :], tiles
+        )
+        w = (-3.0 * (1.0 - VOID)) * d * d * energy * scale
+        for t, (i, jt, h) in enumerate(tiles):
+            wx[i + 2, 8 * jt : 8 * jt + 8, 128 * h : 128 * h + 128] = w[:, 128 * t : 128 * t + 128]
         return c_sum + (VOID + d * d * d * (1.0 - VOID)) * energy, v_sum + d
 
     def sweep(h):
-        def body(i, carry):
-            layer(h, i + 1, i + 1, own(i + 1), rz[0, 0])
-            return unit(i, 0, h, *carry)
+        def body(t, carry):
+            for step in (1, 2):
+                layer(h, 2 * t + step, 2 * t + step, own(2 * t + step), rz[0, 0])
+            for jt in range(nt - 1):
+                carry = unit([(2 * t, jt, h), (2 * t + 1, jt, h)], carry)
+            return carry
 
         return body
 
+    def rest(h, carry):
+        layer(h, ni - 1, ni - 1, own(ni - 1), rz[0, 0])
+        todo = [(ni - 2, jt, h) for jt in range(nt - 1)]
+        if h:
+            todo += [(ni - 2, jt, 0) for jt in range((nt - 1) // 2 * 2, nt - 1)]
+        for at in range(0, len(todo) // 2 * 2, 2):
+            carry = unit(todo[at : at + 2], carry)
+        return carry
+
+    line_x = line_sum(me["gx"] * ni + iota((ni, 128), 0), n["gx"] * ni)
+    inv_x[...] = 1.0 / line_x
     loads[3].wait()
     inv[...] = 1.0 / (
         line_sum(me["gy"] * nj + iota((nj, nk), 0), ny * nj)
@@ -306,10 +329,12 @@
     )
     carry = (none8, none8)
     layer(0, 0, 0, own(0), None)
-    carry = lax.fori_loop(0, ni - 1, sweep(0), carry, unroll=5)
+    carry = lax.fori_loop(0, ni // 2 - 1, sweep(0), carry, unroll=7)
+    carry = rest(0, carry)
     arrive(beside)
     layer(1, 0, 0, own(0), rz[0, 0])
-    carry = lax.fori_loop(0, ni - 1, sweep(1), carry, unroll=5)
+    carry = lax.fori_loop(0, ni // 2 - 1, sweep(1), carry, unroll=7)
+    carry = rest(1, carry)
     arrive(below)
 
     def row_pair(h):
@@ -327,15 +352,12 @@
                 line_f[h, 3 * c + m] = sharp(y)
 
     def upper(i, carry):
-        for q in range(1, nq):
-            for h in range(2):
-                carry = unit(i, q, h, *carry)
-        return carry
+        return unit([(i, nt - 1, 0), (i, nt - 1, 1)], carry)
 
     for h in range(2):
         row_pair(h)
     lax.fori_loop(0, ni, own_row, 0, unroll=4)
-    carry = lax.fori_loop(0, ni - 1, upper, carry, unroll=5)
+    carry = lax.fori_loop(0, ni - 1, upper, carry, unroll=ni - 1)
     zlo = zhi = jnp.zeros((nj, 128), F32)
 
     def pack(i, zlo, zhi):
@@ -356,7 +378,7 @@
         zlo, zhi = pack(i, zlo, zhi)
     zsend[0] = zlo
     zsend[1] = zhi
-    hear(known.at[0], everyone - 1 - mine if everyone <= FEW else count(True))
+    hear(known.at[0], jnp.where(lead, 0, 1))
     around = []
     face_swap(around, (-1, 0, 0))
     arrive(far)
@@ -371,9 +393,8 @@
         for c, x in enumerate((row, moved)):
             for h in range(2):
                 next_row(c, m, ni, h, x[:, 128 * h : 128 * h + 128])
-    for q in range(nq):
-        for h in range(2):
-            carry = unit(ni - 1, q, h, *carry)
+    for jt in range(nt):
+        carry = unit([(ni - 1, jt, 0), (ni - 1, jt, 1)], carry)
     c_sum, v_sum = carry
 
     def share(at, value):
@@ -513,7 +534,7 @@
     scratch = [
         displacement.shape, density.shape, stiffness.shape,
         (3, nj, nk), (3, ni, nk), (8, nk), (2, 2, nj, 128), (3, ni, nk), (8, nk), (nj, 128),
-        (2, 3, ni + 1, 2, nj + 8, 128), (2, nj // 16, ni + 1, 8, nk), (2, 6, ni, 128), (2, 6, ni, 128), (nj, nk),
+        (2, 3, ni + 1, 2, nj + 8, 128), (2, nj // 8, ni + 1, 8, 128), (2, 6, ni, 128), (2, 6, ni, 128), (nj, nk), (ni, 128),
     ]
     later = [
         (ni + 4, nj, nk), (ni, 2, nj + 16, 128),
@@ -529,7 +550,7 @@
         in_specs=[hbm] * 3,
         out_specs=(vmem, vmem),
         scratch_shapes=[pltpu.VMEM(shape, F32) for shape in scratch]
-        + [pltpu.VMEM((2, nj // 16, ni + 1, 48, nk), BF16), pltpu.VMEM((192, 256), BF16), pltpu.VMEM((nk, nk), BF16)]
+        + [pltpu.VMEM((2, nj // 8, ni + 1, 48, 128), BF16), pltpu.VMEM((192, 256), BF16), pltpu.VMEM((nk, nk), BF16)]
         + [pltpu.VMEM(shape, F32) for shape in later]
         + [pltpu.SemaphoreType.DMA((count,)) for count in (4, 7, 7, 26, 26, 2, 2)]
         + [pltpu.SemaphoreType.REGULAR((1,))],

time: 18.2 us -> 16.9 us (0.929)
  Pallas kernels: 17.5 us -> 16 us
    pallas_call x1, Pallas kernels: 16.6 us -> 15.2 us  [on_device(): pl.pallas_call(functools.partial(kernel, sizes), out_shape=(jax.ShapeDtyp...]
where the time goes in v5:
time: 16.9 us; the launch traced here: 16.6 us
  Pallas kernels  16 us (95%)
  between operations  0.64 us (4%)
    pallas_call x1, Pallas kernels, on_device(): pl.pallas_call(functools.partial(kernel, sizes), out_shape=(jax.ShapeDtyp...  15.2 us
    pallas_call x1, Pallas kernels, on_device(): pl.pallas_call(functools.partial(last_pass, cells), out_shape=(jax.ShapeD...  0.82 us

profile of v5, /device:TPU:0, one launch (start us, length us, event | category | flops | bytes accessed | tf_op | source)
XLA Modules:
  0.0 16.6 jit_solution(9902808969259375777)
XLA Ops:
  0.6 15.2 %shard_map.58 = (f32[16,32,256]{2,1,0:T(8,128)S(1)}, f32[1,128]{1,0:T(1,128)S(1)}) custom-call(f32[3,16,32,256]{3,2,1,0:T(8,128)} %u_hbm.1, f32[16,32,256]{2,1,0:T(8,128)} %rho_hbm.1, f32[24,24]{1,0:T(8,128)} %stiff_hbm.1), custom_call_target="tpu_custom_call" | custom-call | tf_op jit(solution)/shard_map/pallas_call | solution.py:544
  15.8 0.8 %shard_map.59 = (f32[16,32,256]{2,1,0:T(8,128)}, f32[1,1]{1,0:T(1,128)}, f32[1,1]{1,0:T(1,128)}) custom-call(f32[16,32,256]{2,1,0:T(8,128)S(1)} %get-tuple-element.8.field, f32[1,128]{1,0:T(1,128)S(1)} %get-tuple-element.9.totals), custom_call_target="tpu_custom_call" | custom-call | tf_op jit(solution)/shard_map/pallas_call | solution.py:562

commit v6 on v5

--- a/solution.py
+++ b/solution.py
@@ -1,4 +1,6 @@
 import functools
+import itertools
+import math
 
 import jax
 import jax.numpy as jnp
@@ -15,6 +17,7 @@
 BF16 = jnp.bfloat16
 NODE_STEPS = [(a, b, c) for a in (0, 1) for b in (0, 1) for c in (0, 1) if a + b + c]
 FEW = 64
+CHUNKS = 4
 AROUND = [(a, b, c) for a in (-1, 0, 1) for b in (-1, 0, 1) for c in (-1, 0, 1) if a or b or c]
 
 
@@ -61,7 +64,7 @@
     sizes, u_hbm, rho_hbm, stiff_hbm, out, totals,
     u, rho, stiff, rx, ry, rxy, rz, ys, yd, zs,
     field, edge, line_f, line_u, inv, inv_x, parts, weights, band, wx, wy,
-    ysend, corner_send, zsend, rows_in, corner_in, rzz, rzs, yrow,
+    ysend, corner_send, zsend, rows_in, corner_in, rzz, rzs, yrow, tally,
     sums, insem, nsend, nrecv, fsend, frecv, gsend, grecv, known,
 ):
     ni, nj, nk = rho.shape
@@ -72,8 +75,9 @@
     up = {axis: me[axis] < n[axis] - 1 for axis in AXES}
 
     loads = []
-    halves = [(u_hbm.at[:, :, :, at : at + 128], u.at[:, :, :, at : at + 128]) for at in (0, 128)]
-    for at, (src, dst) in enumerate([(stiff_hbm, stiff)] + halves + [(rho_hbm, rho)]):
+    halves = [(u_hbm.at[:, 1:, :, at : at + 128], u.at[:, 1:, :, at : at + 128]) for at in (0, 128)]
+    first = [(u_hbm.at[:, 0], u.at[:, 0]), (stiff_hbm, stiff)]
+    for at, (src, dst) in enumerate(first + halves + [(rho_hbm, rho)]):
         copy = pltpu.make_async_copy(src, dst, insem.at[at])
         copy.start()
         loads.append(copy)
@@ -160,73 +164,87 @@
                 ref[...] = jnp.zeros(ref.shape, F32)
 
 
-    def swap(copies, src, dst, send_sem, recv_sem, step):
+    def swap(src, dst, send_sem, recv_sem, step):
         ids, sends = hop(step)
-        copy = pltpu.make_async_remote_copy(
-            src_ref=src, dst_ref=dst, send_sem=send_sem, recv_sem=recv_sem,
-            device_id=ids, device_id_type=MESH,
-        )
-        copies.append((copy, sends, hop(minus(step))[1]))
 
         @pl.when(sends)
         def _():
-            copy.start()
-
-    def arrive(copies):
-        for copy, _, takes in copies:
-
-            @pl.when(takes)
-            def _():
-                copy.wait_recv()
-
-    def finish(copies):
-        for copy, sends, _ in copies:
-
-            @pl.when(sends)
-            def _():
-                copy.wait_send()
-
-    beside, below, far = [], [], []
+            pltpu.make_async_remote_copy(
+                src_ref=src, dst_ref=dst, send_sem=send_sem, recv_sem=recv_sem,
+                device_id=ids, device_id_type=MESH,
+            ).start()
+
+    def states(axis):
+        if n[axis] == 1:
+            return [((), True)]
+        low, high = down[axis], up[axis]
+        found = [((1,), jnp.logical_not(low)), ((-1,), jnp.logical_not(high))]
+        return found + ([((-1, 1), jnp.logical_and(low, high))] if n[axis] > 2 else [])
+
+    def drain(semaphore, items):
+        for case in itertools.product(*(states(axis) for axis in AXES)):
+            rows = sum(
+                math.prod(shape) // 128
+                for step, shape in items
+                if all(s == 0 or s in ways for s, (ways, _) in zip(step, case))
+            )
+            if rows:
+                flag = jnp.logical_and(jnp.logical_and(case[0][1], case[1][1]), case[2][1])
+
+                @pl.when(flag)
+                def _():
+                    pltpu.make_async_copy(tally.at[0:rows], tally.at[0:rows], semaphore).wait()
+
+    def node_items(steps, sign):
+        return [(tuple(sign * s for s in step), node_route(step)[1].shape) for step in steps]
+
+    def face_items(sign):
+        return [(tuple(sign * s for s in step), face_route(step)[1].shape) for step in AROUND]
+
+    def group_of(step):
+        return 2 if step[0] else (1 if step[1] else 0)
 
     def node_swap(step):
-        a, b, c = step
-        at = NODE_STEPS.index(step)
         src, dst = node_route(step)
-        copies = far if a else (below if b else beside)
-        swap(copies, src, dst, nsend.at[at], nrecv.at[at], minus(step))
-
-    def face_swap(copies, step):
-        at = AROUND.index(step)
+        swap(src, dst, nsend.at[0], nrecv.at[group_of(step)], minus(step))
+
+    def arrive(which):
+        drain(nrecv.at[which], node_items([s for s in NODE_STEPS if group_of(s) == which], 1))
+
+    def face_swap(step):
         src, dst = face_route(step)
-        swap(copies, src, dst, fsend.at[at], frecv.at[at], step)
+        swap(src, dst, fsend.at[0], frecv.at[0], step)
 
     loads[0].wait()
-    weights[...] = band_weights(stiff[...])
-    loads[1].wait()
+    hear(barrier, jnp.where(lead, everyone - 1, lower))
+    node_swap((1, 0, 0))
+
+    @pl.when(lead)
+    def _():
+        def greet(at, carry):
+            pl.semaphore_signal(known.at[0], inc=1, device_id=place(at), device_id_type=MESH)
+            return carry
+
+        lax.fori_loop(0, everyone - 1, greet, 0)
+
+    loads[2].wait()
     lane = iota((nj, 128), 1)
-    packed = jnp.zeros((nj, 128), F32)
+    packed = [jnp.zeros((nj, 128), F32)] * 6
     for at in range(3 * ni):
         column = u[at // ni, at % ni, :, 0:128]
-        packed = jnp.where(lane == at, pltpu.roll(column, at, 1) if at else column, packed)
-    zs[...] = packed
-    loads[2].wait()
+        packed[at % 6] = jnp.where(lane == at, pltpu.roll(column, at, 1) if at else column, packed[at % 6])
+    zs[...] = (packed[0] + packed[1]) + (packed[2] + packed[3]) + (packed[4] + packed[5])
+    loads[3].wait()
     yd[...] = jnp.zeros(yd.shape, F32)
     for m in range(3):
         for i in range(ni):
             ys[m, i : i + 1, :] = u[m, i, 0:1, :]
         yd[m : m + 1, :] = u[m, 0, 0:1, :]
-    hear(barrier, jnp.where(lead, everyone - 1, lower))
     for step in sorted(NODE_STEPS, key=lambda step: (sum(step), step)):
-        node_swap(step)
-
-    @pl.when(lead)
-    def _():
-        def greet(at, carry):
-            pl.semaphore_signal(known.at[0], inc=1, device_id=place(at), device_id_type=MESH)
-            return carry
-
-        lax.fori_loop(0, everyone - 1, greet, 0)
-
+        if step != (1, 0, 0):
+            node_swap(step)
+    loads[1].wait()
+    weights[...] = band_weights(stiff[...])
     clear(up["gx"], rx, rxy, rz.at[1], wx.at[ni + 2 : ni + 4], corner_in.at[1], rzz.at[:, 2])
     clear(up["gy"], ry, rxy, rz.at[:, 1, 0:8], rows_in.at[2:4], corner_in.at[:, 1], rzz.at[:, :, 8 + nj : 16 + nj])
     clear(up["gz"], rz, rzz.at[1])
@@ -322,7 +340,7 @@
 
     line_x = line_sum(me["gx"] * ni + iota((ni, 128), 0), n["gx"] * ni)
     inv_x[...] = 1.0 / line_x
-    loads[3].wait()
+    loads[4].wait()
     inv[...] = 1.0 / (
         line_sum(me["gy"] * nj + iota((nj, nk), 0), ny * nj)
         * line_sum(me["gz"] * nk + iota((nj, nk), 1), nz * nk)
@@ -331,11 +349,11 @@
     layer(0, 0, 0, own(0), None)
     carry = lax.fori_loop(0, ni // 2 - 1, sweep(0), carry, unroll=7)
     carry = rest(0, carry)
-    arrive(beside)
+    arrive(0)
     layer(1, 0, 0, own(0), rz[0, 0])
     carry = lax.fori_loop(0, ni // 2 - 1, sweep(1), carry, unroll=7)
     carry = rest(1, carry)
-    arrive(below)
+    arrive(1)
 
     def row_pair(h):
         for m in range(3):
@@ -356,7 +374,7 @@
 
     for h in range(2):
         row_pair(h)
-    lax.fori_loop(0, ni, own_row, 0, unroll=4)
+    lax.fori_loop(0, ni, own_row, 0, unroll=ni)
     carry = lax.fori_loop(0, ni - 1, upper, carry, unroll=ni - 1)
     zlo = zhi = jnp.zeros((nj, 128), F32)
 
@@ -379,9 +397,7 @@
     zsend[0] = zlo
     zsend[1] = zhi
     hear(known.at[0], jnp.where(lead, 0, 1))
-    around = []
-    face_swap(around, (-1, 0, 0))
-    arrive(far)
+    arrive(2)
     for h in range(2):
         layer(h, ni, 0, lambda m, h: rx[m, :, 128 * h : 128 * h + 128], rz[1, 0])
     for m in range(3):
@@ -420,20 +436,19 @@
         return total
 
     def fold(x):
-        row = jnp.sum(x, axis=0, keepdims=True)
-        row = row[:, :128] + row[:, 128:]
-        return row + pltpu.roll(row, 64, 1)
-
-    partial = jnp.where(iota((1, 128), 1) < 64, fold(c_sum), fold(v_sum))
+        return jnp.sum(x[:, :128] + x[:, 128:], axis=0, keepdims=True)
+
+    partial = jnp.concatenate([fold(c_sum), fold(v_sum)], 0)
     share(0, partial)
-    face_swap(around, (1, 0, 0))
+    face_swap((-1, 0, 0))
+    face_swap((1, 0, 0))
 
     zlo, zhi = pack(ni - 1, zsend[0], zsend[1])
     zsend[0] = zlo
     zsend[1] = zhi
     for step in AROUND:
         if step[1] or step[2]:
-            face_swap(around, step)
+            face_swap(step)
 
     def spread_x(i):
         return 3.0 * wx[i + 2] + 2.0 * (wx[i + 1] + wx[i + 3]) + (wx[i] + wx[i + 4])
@@ -455,7 +470,7 @@
         planes_xz(range(first, min(first + 4, ni - 2)))
     for at in range(1, len(stages)):
         share(at, gather(at - 1))
-    arrive(around)
+    drain(frecv.at[0], face_items(-1))
 
     planes_xz((0, 1, ni - 2, ni - 1))
     lines = []
@@ -505,24 +520,24 @@
             else:
                 rim = jnp.where(lane < 2, pltpu.roll(rims[0], 124 - 2 * i, 1), 0.0)
             out[i, :, half] = y + rim
-    for copies in (beside, below, far, around):
-        finish(copies)
+    drain(nsend.at[0], node_items(NODE_STEPS, -1))
+    drain(fsend.at[0], face_items(1))
     totals[...] = gather(len(stages) - 1)
 
 
 def last_pass(cells, field, totals, out, comp, vol, ends, sem):
-    copy = pltpu.make_async_copy(field, out, sem.at[0])
-    copy.start()
-    both = totals[...]
-    first = iota((1, 128), 1) < 64
-    ends[0] = jnp.sum(jnp.where(first, both, 0.0), axis=1, keepdims=True) / cells
-    ends[1] = jnp.sum(jnp.where(first, 0.0, both), axis=1, keepdims=True) / cells
-    small = [pltpu.make_async_copy(ends.at[at], dst, sem.at[1 + at]) for at, dst in enumerate((comp, vol))]
-    for one in small:
-        one.start()
-    for one in small:
-        one.wait()
-    copy.wait()
+    step = field.shape[0] // CHUNKS
+    moves = [(field.at[at * step : at * step + step], out.at[at * step : at * step + step]) for at in range(CHUNKS)]
+    copies = [pltpu.make_async_copy(src, dst, sem.at[at]) for at, (src, dst) in enumerate(moves)]
+    for copy in copies:
+        copy.start()
+    ends[...] = jnp.sum(totals[...], axis=1, keepdims=True)[:, :, None] / cells
+    for at, dst in enumerate((comp, vol)):
+        small = pltpu.make_async_copy(ends.at[at], dst, sem.at[CHUNKS + at])
+        small.start()
+        copies.append(small)
+    for copy in copies:
+        copy.wait()
 
 
 def on_device(sizes, displacement, density, stiffness):
@@ -539,20 +554,21 @@
     later = [
         (ni + 4, nj, nk), (ni, 2, nj + 16, 128),
         (2, 2, ni, nk), (2, 2, 8, nk), (2, nj, 128), (4, ni + 16, nk), (2, 2, 8, nk),
-        (2, 3, nj + 16, 128), (2, nj + 16, 128), (4, ni, nk), (members, 1, 128),
+        (2, 3, nj + 16, 128), (2, nj + 16, 128), (4, ni, nk),
+        (4 * (ni + nj) * nk // 128 + 32 * nk // 128 + 6 * (nj + 16), 128), (members, 2, 128),
     ]
     field, totals = pl.pallas_call(
         functools.partial(kernel, sizes),
         out_shape=(
             jax.ShapeDtypeStruct((ni, nj, nk), F32),
-            jax.ShapeDtypeStruct((1, 128), F32),
+            jax.ShapeDtypeStruct((2, 128), F32),
         ),
         in_specs=[hbm] * 3,
         out_specs=(vmem, vmem),
         scratch_shapes=[pltpu.VMEM(shape, F32) for shape in scratch]
         + [pltpu.VMEM((2, nj // 8, ni + 1, 48, 128), BF16), pltpu.VMEM((192, 256), BF16), pltpu.VMEM((nk, nk), BF16)]
         + [pltpu.VMEM(shape, F32) for shape in later]
-        + [pltpu.SemaphoreType.DMA((count,)) for count in (4, 7, 7, 26, 26, 2, 2)]
+        + [pltpu.SemaphoreType.DMA((count,)) for count in (5, 1, 3, 1, 1, 2, 2)]
         + [pltpu.SemaphoreType.REGULAR((1,))],
         compiler_params=pltpu.CompilerParams(
             collective_id=0, has_side_effects=True, vmem_limit_bytes=24 * 1024 * 1024
@@ -568,7 +584,7 @@
         ),
         in_specs=[vmem] * 2,
         out_specs=(hbm, hbm, hbm),
-        scratch_shapes=[pltpu.VMEM((2, 1, 1), F32), pltpu.SemaphoreType.DMA((3,))],
+        scratch_shapes=[pltpu.VMEM((2, 1, 1), F32), pltpu.SemaphoreType.DMA((CHUNKS + 2,))],
         compiler_params=pltpu.CompilerParams(vmem_limit_bytes=24 * 1024 * 1024),
     )(field, totals)
     return filtered, comp.reshape(()), vol.reshape(())

time: 16.9 us -> 16.4 us (0.970)
  Pallas kernels: 16 us -> 15.6 us
    pallas_call x1, Pallas kernels: 15.2 us -> 14.8 us  [on_device(): pl.pallas_call(functools.partial(kernel, sizes), out_shape=(jax.ShapeDtyp...]
where the time goes in v6:
time: 16.4 us; the launch traced here: 16.3 us
  Pallas kernels  15.6 us (95%)
  between operations  0.64 us (4%)
    pallas_call x1, Pallas kernels, on_device(): pl.pallas_call(functools.partial(kernel, sizes), out_shape=(jax.ShapeDtyp...  14.8 us
    pallas_call x1, Pallas kernels, on_device(): pl.pallas_call(functools.partial(last_pass, cells), out_shape=(jax.ShapeD...  0.84 us

profile of v6, /device:TPU:0, one launch (start us, length us, event | category | flops | bytes accessed | tf_op | source)
XLA Modules:
  0.0 16.3 jit_solution(14366530125231586737)
XLA Ops:
  0.6 14.8 %shard_map.58 = (f32[16,32,256]{2,1,0:T(8,128)S(1)}, f32[2,128]{1,0:T(2,128)S(1)}) custom-call(f32[3,16,32,256]{3,2,1,0:T(8,128)} %u_hbm.1, f32[16,32,256]{2,1,0:T(8,128)} %rho_hbm.1, f32[24,24]{1,0:T(8,128)} %stiff_hbm.1), custom_call_target="tpu_custom_call" | custom-call | tf_op jit(solution)/shard_map/pallas_call | solution.py:560
  15.4 0.8 %shard_map.59 = (f32[16,32,256]{2,1,0:T(8,128)}, f32[1,1]{1,0:T(1,128)}, f32[1,1]{1,0:T(1,128)}) custom-call(f32[16,32,256]{2,1,0:T(8,128)S(1)} %get-tuple-element.8.field, f32[2,128]{1,0:T(2,128)S(1)} %get-tuple-element.9.totals), custom_call_target="tpu_custom_call" | custom-call | tf_op jit(solution)/shard_map/pallas_call | solution.py:578

commit v7 on v6

--- a/solution.py
+++ b/solution.py
@@ -64,7 +64,7 @@
     sizes, u_hbm, rho_hbm, stiff_hbm, out, totals,
     u, rho, stiff, rx, ry, rxy, rz, ys, yd, zs,
     field, edge, line_f, line_u, inv, inv_x, parts, weights, band, wx, wy,
-    ysend, corner_send, zsend, rows_in, corner_in, rzz, rzs, yrow, tally,
+    ysend, corner_send, zsend, xz_send, rows_in, corner_in, rzz, xz_in, rzs, yrow, tally,
     sums, insem, nsend, nrecv, fsend, frecv, gsend, grecv, known,
 ):
     ni, nj, nk = rho.shape
@@ -146,10 +146,12 @@
     def face_route(step):
         a, b, c = step
         hi_a, hi_b, hi_c = a > 0, b > 0, c > 0
+        if a and c:
+            return xz_send.at[int(hi_a), int(hi_c)], xz_in.at[1 - hi_c, 1 - hi_a, 1 - b]
         if c:
             rows = (slice(nj - 8, nj), slice(0, nj), slice(0, 8))[1 - b]
             to = (slice(0, 8), slice(8, 8 + nj), slice(8 + nj, 16 + nj))[1 - b]
-            return zsend.at[int(hi_c), rows], rzz.at[1 - hi_c, 1 - a, to]
+            return zsend.at[int(hi_c), rows], rzz.at[1 - hi_c, to]
         if a and b:
             return corner_send.at[int(hi_a), int(hi_b)], corner_in.at[1 - hi_a, 1 - hi_b]
         if b:
@@ -211,8 +213,10 @@
     def arrive(which):
         drain(nrecv.at[which], node_items([s for s in NODE_STEPS if group_of(s) == which], 1))
 
-    def face_swap(step):
+    def face_swap(step, rows=None):
         src, dst = face_route(step)
+        if rows is not None:
+            src, dst = src.at[:, rows], dst.at[:, rows]
         swap(src, dst, fsend.at[0], frecv.at[0], step)
 
     loads[0].wait()
@@ -245,12 +249,12 @@
             node_swap(step)
     loads[1].wait()
     weights[...] = band_weights(stiff[...])
-    clear(up["gx"], rx, rxy, rz.at[1], wx.at[ni + 2 : ni + 4], corner_in.at[1], rzz.at[:, 2])
-    clear(up["gy"], ry, rxy, rz.at[:, 1, 0:8], rows_in.at[2:4], corner_in.at[:, 1], rzz.at[:, :, 8 + nj : 16 + nj])
-    clear(up["gz"], rz, rzz.at[1])
-    clear(down["gx"], wx.at[0:2], corner_in.at[0], rzz.at[:, 0])
-    clear(down["gy"], rows_in.at[0:2], corner_in.at[:, 0], rzz.at[:, :, 0:8])
-    clear(down["gz"], rzz.at[0])
+    clear(up["gx"], rx, rxy, rz.at[1], wx.at[ni + 2 : ni + 4], corner_in.at[1], xz_in.at[:, 1])
+    clear(up["gy"], ry, rxy, rz.at[:, 1, 0:8], rows_in.at[2:4], corner_in.at[:, 1], rzz.at[:, 8 + nj : 16 + nj], xz_in.at[:, :, 2])
+    clear(up["gz"], rz, rzz.at[1], xz_in.at[1])
+    clear(down["gx"], wx.at[0:2], corner_in.at[0], xz_in.at[:, 0])
+    clear(down["gy"], rows_in.at[0:2], corner_in.at[:, 0], rzz.at[:, 0:8], xz_in.at[:, :, 0])
+    clear(down["gz"], rzz.at[0], xz_in.at[0])
     apart = jnp.abs(iota((nk, nk), 0) - iota((nk, nk), 1))
     band[...] = jnp.maximum(3 - apart, 0).astype(F32).astype(BF16)
     edge[...] = jnp.zeros(edge.shape, F32)
@@ -353,6 +357,8 @@
     layer(1, 0, 0, own(0), rz[0, 0])
     carry = lax.fori_loop(0, ni // 2 - 1, sweep(1), carry, unroll=7)
     carry = rest(1, carry)
+    ready = slice(0, nj - 8)
+    face_swap((-1, 0, 0), ready)
     arrive(1)
 
     def row_pair(h):
@@ -440,12 +446,20 @@
 
     partial = jnp.concatenate([fold(c_sum), fold(v_sum)], 0)
     share(0, partial)
-    face_swap((-1, 0, 0))
+    face_swap((-1, 0, 0), slice(nj - 8, nj))
     face_swap((1, 0, 0))
 
     zlo, zhi = pack(ni - 1, zsend[0], zsend[1])
     zsend[0] = zlo
     zsend[1] = zhi
+    for top in range(2):
+        for side, z in enumerate((zlo, zhi)):
+            tile = jnp.zeros((8, 128), F32)
+            for jt in range(nt):
+                turn = (4 * jt - (2 * ni if top else 4)) % 128
+                z_at = z[8 * jt : 8 * jt + 8]
+                tile = jnp.where(lane[0:8] >> 2 == jt, pltpu.roll(z_at, turn, 1) if turn else z_at, tile)
+            xz_send[top, side] = tile
     for step in AROUND:
         if step[1] or step[2]:
             face_swap(step)
@@ -489,11 +503,16 @@
     even = lax.rem(lane, 2) == 0
     rims = []
     for side in range(2):
-        x = jnp.where(
-            wide < 4,
-            pltpu.roll(rzz[side, 0], 128 - 2 * ni, 1),
-            jnp.where(wide < 2 * ni + 4, rzz[side, 1], pltpu.roll(rzz[side, 2], 2 * ni, 1)),
-        )
+        outer = []
+        for top in range(2):
+            tiles = [(0, nt - 1)] + [(1, jt) for jt in range(nt)] + [(2, 0)]
+            turns = [((2 * ni + 4 if top else 0) - 4 * jt) % 128 for _, jt in tiles]
+            sources = [xz_in[side, top, slot] for slot, _ in tiles]
+            outer.append(
+                jnp.concatenate([pltpu.roll(x, turn, 1) if turn else x for x, turn in zip(sources, turns)], 0)
+            )
+        inner = jnp.where(wide < 2 * ni + 4, rzz[side], 0.0)
+        x = jnp.where(wide < 4, outer[0], jnp.where((wide >= 2 * ni + 4) & (wide < 2 * ni + 8), outer[1], inner))
         x = (
             3.0 * x
             + 2.0 * (pltpu.roll(x, 2, 1) + pltpu.roll(x, 126, 1))
@@ -553,8 +572,8 @@
     ]
     later = [
         (ni + 4, nj, nk), (ni, 2, nj + 16, 128),
-        (2, 2, ni, nk), (2, 2, 8, nk), (2, nj, 128), (4, ni + 16, nk), (2, 2, 8, nk),
-        (2, 3, nj + 16, 128), (2, nj + 16, 128), (4, ni, nk),
+        (2, 2, ni, nk), (2, 2, 8, nk), (2, nj, 128), (2, 2, 8, 128), (4, ni + 16, nk), (2, 2, 8, nk),
+        (2, nj + 16, 128), (2, 2, 3, 8, 128), (2, nj + 16, 128), (4, ni, nk),
         (4 * (ni + nj) * nk // 128 + 32 * nk // 128 + 6 * (nj + 16), 128), (members, 2, 128),
     ]
     field, totals = pl.pallas_call(

time: 16.4 us -> 15.8 us (0.963)
  Pallas kernels: 15.6 us -> 15 us
    pallas_call x1, Pallas kernels: 14.8 us -> 14.1 us  [on_device(): pl.pallas_call(functools.partial(kernel, sizes), out_shape=(jax.ShapeDtyp...]
where the time goes in v7:
time: 15.8 us; the launch traced here: 15.6 us
  Pallas kernels  15 us (95%)
  between operations  0.64 us (4%)
    pallas_call x1, Pallas kernels, on_device(): pl.pallas_call(functools.partial(kernel, sizes), out_shape=(jax.ShapeDtyp...  14.1 us
    pallas_call x1, Pallas kernels, on_device(): pl.pallas_call(functools.partial(last_pass, cells), out_shape=(jax.ShapeD...  0.84 us

profile of v7, /device:TPU:0, one launch (start us, length us, event | category | flops | bytes accessed | tf_op | source)
XLA Modules:
  0.0 15.6 jit_solution(18151731226319675640)
XLA Ops:
  0.6 14.1 %shard_map.58 = (f32[16,32,256]{2,1,0:T(8,128)S(1)}, f32[2,128]{1,0:T(2,128)S(1)}) custom-call(f32[3,16,32,256]{3,2,1,0:T(8,128)} %u_hbm.1, f32[16,32,256]{2,1,0:T(8,128)} %rho_hbm.1, f32[24,24]{1,0:T(8,128)} %stiff_hbm.1), custom_call_target="tpu_custom_call" | custom-call | tf_op jit(solution)/shard_map/pallas_call | solution.py:579
  14.8 0.8 %shard_map.59 = (f32[16,32,256]{2,1,0:T(8,128)}, f32[1,1]{1,0:T(1,128)}, f32[1,1]{1,0:T(1,128)}) custom-call(f32[16,32,256]{2,1,0:T(8,128)S(1)} %get-tuple-element.8.field, f32[2,128]{1,0:T(2,128)S(1)} %get-tuple-element.9.totals), custom_call_target="tpu_custom_call" | custom-call | tf_op jit(solution)/shard_map/pallas_call | solution.py:597
